TPU v7x, 32 devices: a whole 2x2x4 slice. The times are simulated.
32 devices in a mesh: gx: 4 (over y, x), gy: 8 (over z, core).
Axes of the slice: x: 2, y: 2, z: 4, core: 2. Of those that a mesh axis runs over, the one named last changes fastest.
Arguments:
- value_field: float32 [4, 24, 48, 1536], P(None, 'gx', 'gy'), may hold values from -16 to 17
- target_mask: int32 [4, 24, 48, 1536], P(None, 'gx', 'gy'), may hold values 0 or 1
- obstacle_mask: int32 [4, 24, 48, 1536], P(None, 'gx', 'gy'), may hold values 0 or 1
- drift_gains: float32 [5], replicated, may hold values from 0.5 to 2
- control_costs: float32 [5], replicated, may hold values from 0.25 to 1
Outputs:
- reach_value: float32 [4, 24, 48, 1536], P(None, 'gx', 'gy')
- time_steps: float32 [3], replicated
All inputs are finite; a program needn't handle non-finite values. No bound on the sum of `target_mask` or of `obstacle_mask` on one device may be relied on, other than what follows from the above.
Results may differ from a plain program's by a relative error of at most 0.0003.
Values sent between devices are 32-bit elements; how exact they have to be, the bound alone decides.
A program may use at most 128 MiB of HBM per device.

v0:
```python
import functools
import math

import jax
import jax.numpy as jnp
from jax import lax
from jax.experimental import pallas as pl
from jax.experimental.pallas import tpu as pltpu
from jax.sharding import PartitionSpec as P

N3 = 32
N4 = 48
GRID = 96
STEPS = 3
COURANT = 0.5
EPS = 0.75e-6
LANES = 8 * N4


def wave(vs):
    n = len(vs) - 6
    d = [vs[k + 1] - vs[k] for k in range(n + 5)]
    f = [d[k + 1] - d[k] for k in range(n + 4)]
    e = [f[k + 1] - f[k] for k in range(n + 3)]
    j = [e[k + 1] - e[k] for k in range(n + 2)]
    k15 = [1.5 * x for x in f]
    base = [e[k] * e[k] + (0.5 * k15[k] * f[k + 1] + EPS) for k in range(n + 3)]
    left, mid, right = [], [], []
    for k in range(n + 1):
        a = base[k] + k15[k + 1] * e[k]
        b = base[k + 1]
        c = base[k + 2] - k15[k + 2] * e[k + 2]
        left.append(a * a)
        mid.append(b * b)
        right.append(c * c)
    low, high = [], []
    for k in range(n + 1):
        bc = mid[k] * right[k]
        ab = left[k] * mid[k]
        ac = 6.0 * (left[k] * right[k])
        n1 = bc * j[k]
        n2 = ab * j[k + 1]
        total = bc + ab
        both = n1 + n2
        both = both + both
        core = total + ac
        low.append((both + n2) / (core + (ab + ab)) if k < n else None)
        high.append((both + n1) / (core + (bc + bc)) if k > 0 else None)
    out = []
    for i in range(n):
        rm, rp = low[i], high[i + 1]
        center = 6.0 * (vs[i + 4] - vs[i + 2])
        middle = center - (e[i + 1] + e[i + 2]) + (rp - rm)
        jump = (rp + rm) - j[i + 1]
        out.append((middle, jump))
    return out


def tally(middle, jump, drift, kappa):
    gap = drift - middle
    return jnp.abs(gap) + jnp.abs(jump), (kappa * middle) * (drift + gap)


def unsplit_kernel(kappa_ref, v_ref, f0_ref, f3_ref, f4_ref, h_ref, q_ref, peak_ref, up_ref):
    planes, rows, cols, width = v_ref.shape
    lane = lax.broadcasted_iota(jnp.int32, (1, width), 1)
    third, fourth = lane // N4, lane % N4
    peak_ref[...] = jnp.zeros_like(peak_ref)

    def per_row(r, carry):
        def shift(p, carry):
            v = v_ref[p, r]
            for base, stride, place, extent in ((0, N4, third, width // N4), (6, 1, fourth, N4)):
                now = v
                for s in range(1, 4):
                    now = jnp.where(place + s < extent, pltpu.roll(v, width - s * stride, 1), now)
                    up_ref[base + 2 + s, p] = now
                now = v
                for s in range(1, 4):
                    now = jnp.where(place >= s, pltpu.roll(v, s * stride, 1), now)
                    up_ref[base + 3 - s, p] = now
            return carry

        lax.fori_loop(0, planes, shift, 0)

        def along_planes(g, carry):
            at = pl.ds(pl.multiple_of(g * 128, 128), 128)
            vs = [v_ref[p, r, :, at] for p in range(planes)]
            drift = f0_ref[r, :, at]
            top = peak_ref[0, :, at]
            cells = wave([vs[0]] * 3 + vs + [vs[-1]] * 3)
            for p in range(planes):
                speed, part = tally(*cells[p], drift, kappa_ref[0])
                top = jnp.maximum(top, speed)
                h_ref[p, r, :, at] = part
                q_ref[0, p, r, :, at] = cells[p][1]
            peak_ref[0, :, at] = top
            return carry

        lax.fori_loop(0, width // 128, along_planes, 0)

        def per_group(g, carry):
            at = pl.ds(pl.multiple_of(g * LANES, 128), LANES)

            def per_plane(p, carry):
                v = v_ref[p, r, :, at]
                total = h_ref[p, r, :, at]
                for slot, base, number in ((1, 0, 3), (2, 6, 4)):
                    around = [up_ref[base + k, p, :, at] for k in range(6)]
                    ((middle, jump),) = wave(around[:3] + [v] + around[3:])
                    drift = f3_ref[p, :, :] if number == 3 else f4_ref[r, :, at]
                    speed, part = tally(middle, jump, drift, kappa_ref[number])
                    peak_ref[slot, :, at] = jnp.maximum(peak_ref[slot, :, at], speed)
                    q_ref[slot, p, r, :, at] = jump
                    total = total + part
                h_ref[p, r, :, at] = total
                return carry

            lax.fori_loop(0, planes, per_plane, 0)
            return carry

        lax.fori_loop(0, width // LANES, per_group, 0)
        return carry

    lax.fori_loop(0, rows, per_row, 0)


def split_kernel(
    kappa_ref, v_ref, a_lo, a_hi, b_lo, b_hi, f1_ref, f2_ref, hin_ref, peak_un_ref,
    h_ref, q_ref, top_ref, ext_ref, near_ref, peak_ref,
):
    planes, rows, cols, width = v_ref.shape
    peak_ref[...] = jnp.zeros_like(peak_ref)

    def per_plane(p, carry):
        def fill(r, carry):
            ext_ref[0:3, :] = b_lo[p, r]
            ext_ref[3 : 3 + cols, :] = v_ref[p, r]
            ext_ref[3 + cols : 6 + cols, :] = b_hi[p, r]
            for k in range(7):
                near_ref[k, r] = ext_ref[k : k + cols, :]
            return carry

        lax.fori_loop(0, rows, fill, 0)

        def along_rows(g, carry):
            at = pl.ds(pl.multiple_of(g * 128, 128), 128)
            vs = [a_lo[p, k, :, at] for k in range(3)]
            vs += [v_ref[p, r, :, at] for r in range(rows)]
            vs += [a_hi[p, k, :, at] for k in range(3)]
            top = peak_ref[0, :, at]
            drift = f1_ref[p, :, at]
            for r, (middle, jump) in enumerate(wave(vs)):
                speed, part = tally(middle, jump, drift, kappa_ref[1])
                top = jnp.maximum(top, speed)
                h_ref[p, r, :, at] = hin_ref[p, r, :, at] + part
                q_ref[0, p, r, :, at] = jump
            peak_ref[0, :, at] = top
            return carry

        lax.fori_loop(0, width // 128, along_rows, 0)

        def per_group(g, carry):
            at = pl.ds(pl.multiple_of(g * LANES, 128), LANES)

            def per_row(r, carry):
                ((middle, jump),) = wave([near_ref[k, r, :, at] for k in range(7)])
                speed, part = tally(middle, jump, f2_ref[r, :, at], kappa_ref[2])
                peak_ref[1, :, at] = jnp.maximum(peak_ref[1, :, at], speed)
                h_ref[p, r, :, at] = h_ref[p, r, :, at] + part
                q_ref[1, p, r, :, at] = jump
                return carry

            lax.fori_loop(0, rows, per_row, 0)
            return carry

        lax.fori_loop(0, width // LANES, per_group, 0)
        return carry

    lax.fori_loop(0, planes, per_plane, 0)
    tops = [peak_un_ref[0], peak_ref[0], peak_ref[1], peak_un_ref[1], peak_un_ref[2]]
    row = lax.broadcasted_iota(jnp.int32, top_ref.shape, 0)
    out = jnp.zeros(top_ref.shape, jnp.float32)
    for number, part in enumerate(tops):
        out = jnp.where(row == number, jnp.max(part), out)
    top_ref[...] = out


def peak_kernel(sizes, own_ref, out_ref, slots, send_sem, recv_sem):
    nx, ny = sizes
    n = nx * ny
    me = lax.axis_index("gx") * ny + lax.axis_index("gy")

    def place(k):
        other = (me + k) % n
        return (other // ny, other % ny)

    barrier = pltpu.get_barrier_semaphore()

    def greet(k, carry):
        pl.semaphore_signal(
            barrier, inc=1, device_id=place(k), device_id_type=pl.DeviceIdType.MESH
        )
        return carry

    lax.fori_loop(1, n, greet, 0)
    pl.semaphore_wait(barrier, n - 1)

    def copy(k):
        return pltpu.make_async_remote_copy(
            src_ref=own_ref,
            dst_ref=slots.at[k],
            send_sem=send_sem.at[k],
            recv_sem=recv_sem.at[k],
            device_id=place(k),
            device_id_type=pl.DeviceIdType.MESH,
        )

    def send(k, carry):
        copy(k).start()
        return carry

    lax.fori_loop(1, n, send, 0)

    def take(k, top):
        copy(k).wait_recv()
        return jnp.maximum(top, slots[k])

    out_ref[...] = lax.fori_loop(1, n, take, own_ref[...])

    def finish(k, carry):
        copy(k).wait_send()
        return carry

    lax.fori_loop(1, n, finish, 0)


def peak_everywhere(own):
    sizes = (lax.axis_size("gx"), lax.axis_size("gy"))
    n = sizes[0] * sizes[1]
    return pl.pallas_call(
        functools.partial(peak_kernel, sizes),
        out_shape=jax.ShapeDtypeStruct(own.shape, jnp.float32),
        in_specs=[VMEM],
        out_specs=VMEM,
        scratch_shapes=[
            pltpu.VMEM((n,) + own.shape, jnp.float32),
            pltpu.SemaphoreType.DMA((n,)),
            pltpu.SemaphoreType.DMA((n,)),
        ],
        compiler_params=pltpu.CompilerParams(collective_id=0, has_side_effects=True),
    )(own)


def move_kernel(scale_ref, v_ref, h_ref, qu_ref, qs_ref, target_ref, obstacle_ref, out_ref):
    planes, rows, cols, width = v_ref.shape

    def per_cell(i, carry):
        p, r = i // rows, i % rows
        change = scale_ref[0] * h_ref[p, r]
        change = change - scale_ref[1] * qu_ref[0, p, r] - scale_ref[2] * qs_ref[0, p, r]
        change = change - scale_ref[3] * qs_ref[1, p, r] - scale_ref[4] * qu_ref[1, p, r]
        change = change - scale_ref[5] * qu_ref[2, p, r]
        new = v_ref[p, r] - change
        new = jnp.where(target_ref[p, r] == 1, jnp.minimum(new, -0.5), new)
        out_ref[p, r] = jnp.where(obstacle_ref[p, r] == 1, jnp.maximum(new, 0.5), new)
        return carry

    lax.fori_loop(0, planes * rows, per_cell, 0)


VMEM = pl.BlockSpec(memory_space=pltpu.VMEM)
SMEM = pl.BlockSpec(memory_space=pltpu.SMEM)


def call(kernel, ins, outs, scratch, flops, args):
    return pl.pallas_call(
        kernel,
        out_shape=[jax.ShapeDtypeStruct(s, jnp.float32) for s in outs],
        in_specs=[SMEM] + [VMEM] * ins,
        out_specs=[VMEM] * len(outs),
        scratch_shapes=scratch,
        cost_estimate=pl.CostEstimate(flops=flops, bytes_accessed=1 << 20, transcendentals=0),
        compiler_params=pltpu.CompilerParams(vmem_limit_bytes=40 << 20),
    )(*args)


def drifts(shape, gains):
    planes, rows, cols, width = shape
    one = 2.0 * math.pi / (rows * lax.axis_size("gx"))
    two = 2.0 * math.pi / (cols * lax.axis_size("gy"))
    row = lax.axis_index("gx") * rows + jnp.arange(rows, dtype=jnp.int32)
    col = lax.axis_index("gy") * cols + jnp.arange(cols, dtype=jnp.int32)
    first = (jnp.arange(planes, dtype=jnp.float32) - planes / 2 + 0.5) * (2.0 / GRID)
    a = (one * row.astype(jnp.float32)).reshape(rows, 1, 1)
    b = (two * col.astype(jnp.float32)).reshape(1, cols, 1)
    lane = jnp.arange(width, dtype=jnp.int32)
    third = ((lane // N4).astype(jnp.float32) - N3 / 2 + 0.5) * (2.0 / GRID)
    fourth = ((lane % N4).astype(jnp.float32) - N4 / 2 + 0.5) * (2.0 / GRID)
    third, fourth = third.reshape(1, 1, -1), fourth.reshape(1, 1, -1)
    x0 = first.reshape(planes, 1, 1)
    f3 = gains[3] * (jnp.sin(b) - x0)
    return [
        gains[0] * (jnp.cos(a) - 0.5 * jnp.cos(b) + third),
        gains[1] * (fourth - 0.3 * x0),
        gains[2] * (third + 0.5 * jnp.sin(a)),
        jnp.broadcast_to(f3, (planes, cols, LANES)),
        gains[4] * (jnp.cos(a) * jnp.sin(b) - fourth),
    ]


def exchange(part_lo, part_hi, axis):
    devices = lax.axis_size(axis)
    up = [(i, (i + 1) % devices) for i in range(devices)]
    down = [(k, i) for i, k in up]
    return lax.ppermute(part_hi, axis, up), lax.ppermute(part_lo, axis, down)


def body(value, target, obstacle, gains, costs):
    shape = value.shape
    planes, rows, cols, width = shape
    h = jnp.array(
        [
            2.0 / GRID,
            2.0 * math.pi / (rows * lax.axis_size("gx")),
            2.0 * math.pi / (cols * lax.axis_size("gy")),
            2.0 / GRID,
            2.0 / GRID,
        ],
        dtype=jnp.float32,
    )
    kappa = costs / (288.0 * h)
    f = [d * (12.0 / costs[i]) for i, d in enumerate(drifts(shape, gains))]
    steps = []
    for _ in range(STEPS):
        a_lo, a_hi = exchange(value[:, :3], value[:, -3:], "gx")
        b_lo, b_hi = exchange(value[:, :, :3], value[:, :, -3:], "gy")
        part, q_un, peak_un = call(
            unsplit_kernel,
            4,
            [shape, (3,) + shape, (3, cols, width)],
            [pltpu.VMEM((12, planes, cols, width), jnp.float32)],
            1 << 28,
            (kappa, value, f[0], f[3], f[4]),
        )
        part, q_sp, top = call(
            split_kernel,
            9,
            [shape, (2,) + shape, (8, 128)],
            [
                pltpu.VMEM((cols + 6, width), jnp.float32),
                pltpu.VMEM((7, rows, cols, width), jnp.float32),
                pltpu.VMEM((2, cols, width), jnp.float32),
            ],
            1 << 27,
            (kappa, value, a_lo, a_hi, b_lo, b_hi, f[1], f[2], part, peak_un),
        )
        bounds = peak_everywhere(top)[:5, 0] * (costs / 12.0)
        dt = COURANT / (jnp.sum(bounds / h) + 1e-6)
        scales = jnp.concatenate([dt[None], dt * bounds / (12.0 * h)])
        (value,) = call(
            move_kernel, 6, [shape], [], 1 << 24,
            (scales, value, part, q_un, q_sp, target, obstacle),
        )
        steps.append(dt)
    return value, jnp.stack(steps)


def solution(mesh):
    spec = P(None, "gx", "gy", None)
    return jax.shard_map(
        body,
        mesh=mesh,
        in_specs=(spec, spec, spec, P(), P()),
        out_specs=(spec, P()),
        check_vma=False,
    )
```

profile of v0, /device:TPU:0, one launch (start us, length us, event | category | flops | bytes accessed | tf_op | source)
XLA Modules:
  0.0 214.2 jit_solution(16312122386508826428)
XLA Ops:
  0.6 2.2 %fusion.23 = (f32[4,3,6,1536]{3,0,2,1:T(4,128)}, f32[4,3,6,1536]{3,0,2,1:T(4,128)}) fusion(f32[4,6,6,1536]{3,0,2,1:T(4,128)} %param.6), kind=kLoop, calls=%fused_computation.54 | loop fusion | bytes 1769472 | tf_op jit(solution)/shard_map/slice | solution.py:336
  2.8 3.9 %collective-permute-start.1 = (f32[4,3,6,1536]{3,0,2,1:T(4,128)}, f32[4,3,6,1536]{3,0,2,1:T(4,128)}, u32[]{:S(2)}, u32[]{:S(2)}) collective-permute-start(f32[4,3,6,1536]{3,0,2,1:T(4,128)} %get-tuple-element.54), channel_id=1, source_target_pairs={{8,0},{16,8},{24,16},{0,24},{9,1},{17,9},{25,17},{1,25},{10,2},{18... | collective-permute-start | bytes 1327112 | tf_op jit(solution)/shard_map/ppermute | solution.py:316
  6.8 1.0 fusion.22
  7.8 2.8 %collective-permute-start.3 = (f32[4,6,3,1536]{3,0,2,1:T(4,128)}, f32[4,6,3,1536]{3,0,2,1:T(4,128)}, u32[]{:S(2)}, u32[]{:S(2)}) collective-permute-start(f32[4,6,3,1536]{3,0,2,1:T(4,128)} %get-tuple-element.52), channel_id=1, source_target_pairs={{1,0},{2,1},{3,2},{4,3},{5,4},{6,5},{7,6},{0,7},{9,8},{10,9},{11,1... | collective-permute-start | bytes 1327112 | tf_op jit(solution)/shard_map/ppermute | solution.py:316
  11.6 0.6 fusion.12
  12.8 0.6 fusion.2
  13.7 0.8 fusion.25
  14.6 0.7 fusion.24
  18.6 1.5 copy.43.target_ref
  20.1 1.5 copy.44.obstacle_ref
  21.7 0.6 multiply_multiply_fusion.4
  22.3 0.8 multiply_multiply_fusion.2.f2_ref
  23.1 0.7 multiply_multiply_fusion.1.f0_ref
  23.9 0.7 multiply_multiply_fusion.f4_ref
  24.7 18.3 %shard_map.77 = (f32[4,6,6,1536]{3,2,1,0:T(8,128)S(1)}, f32[3,4,6,6,1536]{4,3,2,1,0:T(8,128)S(1)}, f32[3,6,1536]{2,1,0:T(8,128)S(1)}) custom-call(f32[5]{0:T(128)S(1)} %multiply.6.kappa_ref, f32[4,6,6,1536]{3,2,1,0:T(8,128)S(1)} %copy.37.v_ref, f32[6,6,1536]{2,1,0:T(8,128)S(1)} %multiply_multiply_fusion.1.f0_ref, f32[4,6,384]{2,1,0:T(8,128)S(1)} %broadcast_in_dim.14.f3_ref, ...), custom_call_target="tpu_custom_call" | custom-call | flops 268435456 | bytes 1048576 | tf_op jit(solution)/shard_map/pallas_call | solution.py:277
  43.0 1.7 copy-done.13
  44.8 0.7 multiply_multiply_fusion.3.f1_ref
  45.5 1.2 copy.39.a_hi
  46.7 1.2 copy.38.a_lo
  47.9 1.2 copy.41.b_hi
  49.2 1.2 copy.40.b_lo
  50.5 10.4 %shard_map.78 = (f32[4,6,6,1536]{3,2,1,0:T(8,128)S(1)}, f32[2,4,6,6,1536]{4,3,2,1,0:T(8,128)S(1)}, f32[8,128]{1,0:T(8,128)S(1)}) custom-call(f32[5]{0:T(128)S(1)} %multiply.6.kappa_ref, f32[4,6,6,1536]{3,2,1,0:T(8,128)S(1)} %copy.37.v_ref, f32[4,3,6,1536]{3,2,1,0:T(8,128)S(1)} %copy.38.a_lo, f32[4,3,6,1536]{3,2,1,0:T(8,128)S(1)} %copy.39.a_hi, ...), custom_call_target="tpu_custom_call" | custom-call | flops 134217728 | bytes 1048576 | tf_op jit(solution)/shard_map/pallas_call | solution.py:277
  60.9 1.5 copy-done.19
  62.3 1.0 copy-done.25
  63.9 11.9 %shard_map.79 = f32[8,128]{1,0:T(8,128)} custom-call(f32[8,128]{1,0:T(8,128)} %copy-done.39), custom_call_target="tpu_custom_call" | custom-call | tf_op jit(solution)/shard_map/pallas_call | solution.py:241
  75.8 0.8 slice_reduce_fusion.2
  76.6 1.3 multiply_reduce_fusion.2
  78.7 1.3 copy-done.4
  80.0 2.0 copy-done.14
  82.0 1.7 copy-done.20
  83.6 1.3 copy-done.26
  84.9 1.7 shard_map.80.v_ref
  87.7 3.4 %collective-permute-start.7 = (f32[4,6,3,1536]{3,0,2,1:T(4,128)S(1)}, f32[4,6,3,1536]{3,0,2,1:T(4,128)S(1)}, u32[]{:S(2)}, u32[]{:S(2)}) collective-permute-start(f32[4,6,3,1536]{3,0,2,1:T(4,128)S(1)} %copy.48), channel_id=1, source_target_pairs={{1,0},{2,1},{3,2},{4,3},{5,4},{6,5},{7,6},{0,7},{9,8},{10,9},{11,1... | collective-permute-start | bytes 1327112 | tf_op jit(solution)/shard_map/ppermute | solution.py:316
  91.4 1.4 collective-permute-start.4
  93.1 1.6 collective-permute-start.5
  94.8 18.3 %shard_map.81 = (f32[4,6,6,1536]{3,2,1,0:T(8,128)S(1)}, f32[3,4,6,6,1536]{4,3,2,1,0:T(8,128)S(1)}, f32[3,6,1536]{2,1,0:T(8,128)S(1)}) custom-call(f32[5]{0:T(128)S(1)} %multiply.6.kappa_ref, f32[4,6,6,1536]{3,2,1,0:T(8,128)S(1)} %shard_map.80.v_ref, f32[6,6,1536]{2,1,0:T(8,128)S(1)} %copy-done.6, f32[4,6,384]{2,1,0:T(8,128)S(1)} %copy-done.30, ...), custom_call_target="tpu_custom_call" | custom-call | flops 268435456 | bytes 1048576 | tf_op jit(solution)/shard_map/pallas_call | solution.py:277
  113.1 1.7 copy-done.15
  116.1 10.4 %shard_map.82 = (f32[4,6,6,1536]{3,2,1,0:T(8,128)S(1)}, f32[2,4,6,6,1536]{4,3,2,1,0:T(8,128)S(1)}, f32[8,128]{1,0:T(8,128)S(1)}) custom-call(f32[5]{0:T(128)S(1)} %multiply.6.kappa_ref, f32[4,6,6,1536]{3,2,1,0:T(8,128)S(1)} %shard_map.80.v_ref, f32[4,3,6,1536]{3,2,1,0:T(8,128)S(1)} %copy.49.a_lo, f32[4,3,6,1536]{3,2,1,0:T(8,128)S(1)} %copy.50.a_hi, ...), custom_call_target="tpu_custom_call" | custom-call | flops 134217728 | bytes 1048576 | tf_op jit(solution)/shard_map/pallas_call | solution.py:277
  126.5 1.5 copy-done.21
  127.9 1.1 copy-done.27
  129.6 9.9 %shard_map.83 = f32[8,128]{1,0:T(8,128)} custom-call(f32[8,128]{1,0:T(8,128)} %copy-done.40), custom_call_target="tpu_custom_call" | custom-call | tf_op jit(solution)/shard_map/pallas_call | solution.py:241
  139.6 0.8 slice_reduce_fusion.1
  140.4 0.6 multiply_reduce_fusion.1
  141.7 1.3 copy-done.1
  143.0 2.0 copy-done.16
  145.0 1.7 copy-done.22
  146.7 1.3 copy-done.28
  148.0 1.7 shard_map.84.v_ref
  150.7 3.4 %collective-permute-start.11 = (f32[4,6,3,1536]{3,0,2,1:T(4,128)S(1)}, f32[4,6,3,1536]{3,0,2,1:T(4,128)S(1)}, u32[]{:S(2)}, u32[]{:S(2)}) collective-permute-start(f32[4,6,3,1536]{3,0,2,1:T(4,128)S(1)} %copy.58), channel_id=1, source_target_pairs={{1,0},{2,1},{3,2},{4,3},{5,4},{6,5},{7,6},{0,7},{9,8},{10,9},{11,1... | collective-permute-start | bytes 1327112 | tf_op jit(solution)/shard_map/ppermute | solution.py:316
  154.5 1.1 collective-permute-start.8
  155.9 2.1 collective-permute-start.9
  158.0 18.3 %shard_map.85 = (f32[4,6,6,1536]{3,2,1,0:T(8,128)S(1)}, f32[3,4,6,6,1536]{4,3,2,1,0:T(8,128)S(1)}, f32[3,6,1536]{2,1,0:T(8,128)S(1)}) custom-call(f32[5]{0:T(128)S(1)} %multiply.6.kappa_ref, f32[4,6,6,1536]{3,2,1,0:T(8,128)S(1)} %shard_map.84.v_ref, f32[6,6,1536]{2,1,0:T(8,128)S(1)} %copy-done.7, f32[4,6,384]{2,1,0:T(8,128)S(1)} %copy-done.31, ...), custom_call_target="tpu_custom_call" | custom-call | flops 268435456 | bytes 1048576 | tf_op jit(solution)/shard_map/pallas_call | solution.py:277
  176.3 1.7 copy-done.11
  179.3 10.4 %shard_map.86 = (f32[4,6,6,1536]{3,2,1,0:T(8,128)S(1)}, f32[2,4,6,6,1536]{4,3,2,1,0:T(8,128)S(1)}, f32[8,128]{1,0:T(8,128)S(1)}) custom-call(f32[5]{0:T(128)S(1)} %multiply.6.kappa_ref, f32[4,6,6,1536]{3,2,1,0:T(8,128)S(1)} %shard_map.84.v_ref, f32[4,3,6,1536]{3,2,1,0:T(8,128)S(1)} %copy.59.a_lo, f32[4,3,6,1536]{3,2,1,0:T(8,128)S(1)} %copy.60.a_hi, ...), custom_call_target="tpu_custom_call" | custom-call | flops 134217728 | bytes 1048576 | tf_op jit(solution)/shard_map/pallas_call | solution.py:277
  189.7 1.5 copy-done.17
  191.2 1.1 copy-done.23
  192.8 10.5 %shard_map.87 = f32[8,128]{1,0:T(8,128)} custom-call(f32[8,128]{1,0:T(8,128)} %copy-done.38), custom_call_target="tpu_custom_call" | custom-call | tf_op jit(solution)/shard_map/pallas_call | solution.py:241
  203.3 0.8 slice_reduce_fusion
  204.1 0.6 multiply_reduce_fusion
  206.1 2.0 copy-done.12
  208.1 1.7 copy-done.18
  209.8 1.3 copy-done.24
  211.0 1.7 shard_map.88
  212.7 1.5 copy.65
  (138 shorter events, 10.6 us)
Async XLA Ops:
  0.6 6.1 %copy-start.41 = (f32[4,6,6,1536]{3,0,2,1:T(4,128)S(1)}, f32[4,6,6,1536]{3,0,2,1:T(4,128)}, u32[]{:S(2)}) copy-start(f32[4,6,6,1536]{3,0,2,1:T(4,128)} %param.6) | copy-start | bytes 2654212
  2.8 42.7 %collective-permute-start.1 = (f32[4,3,6,1536]{3,0,2,1:T(4,128)}, f32[4,3,6,1536]{3,0,2,1:T(4,128)}, u32[]{:S(2)}, u32[]{:S(2)}) collective-permute-start(f32[4,3,6,1536]{3,0,2,1:T(4,128)} %get-tuple-element.54), channel_id=1, source_target_pairs={{8,0},{16,8},{24,16},{0,24},{9,1},{17,9},{25,17},{1,25},{10,2},{18... | collective-permute-start | bytes 1327112 | tf_op jit(solution)/shard_map/ppermute | solution.py:316
  6.8 40.0 %collective-permute-start = (f32[4,3,6,1536]{3,0,2,1:T(4,128)}, f32[4,3,6,1536]{3,0,2,1:T(4,128)}, u32[]{:S(2)}, u32[]{:S(2)}) collective-permute-start(f32[4,3,6,1536]{3,0,2,1:T(4,128)} %get-tuple-element.55), channel_id=1, source_target_pairs={{0,8},{8,16},{16,24},{24,0},{1,9},{9,17},{17,25},{25,1},{2,10},{10... | collective-permute-start | bytes 1327112 | tf_op jit(solution)/shard_map/ppermute | solution.py:316
  7.7 6.0 %copy-start.43 = (f32[5]{0:T(128)S(1)}, f32[5]{0:T(128)}, u32[]{:S(2)}) copy-start(f32[5]{0:T(128)} %param.10) | copy-start | bytes 64
  7.8 6.8 %copy-start.52 = (f32[5]{0:T(128)S(1)}, f32[5]{0:T(128)}, u32[]{:S(2)}) copy-start(f32[5]{0:T(128)} %constant.86) | copy-start | bytes 64
  7.8 6.8 %copy-start.44 = (f32[5]{0:T(128)S(1)}, f32[5]{0:T(128)}, u32[]{:S(2)}) copy-start(f32[5]{0:T(128)} %param.9) | copy-start | bytes 64
  7.8 40.1 %collective-permute-start.3 = (f32[4,6,3,1536]{3,0,2,1:T(4,128)}, f32[4,6,3,1536]{3,0,2,1:T(4,128)}, u32[]{:S(2)}, u32[]{:S(2)}) collective-permute-start(f32[4,6,3,1536]{3,0,2,1:T(4,128)} %get-tuple-element.52), channel_id=1, source_target_pairs={{1,0},{2,1},{3,2},{4,3},{5,4},{6,5},{7,6},{0,7},{9,8},{10,9},{11,1... | collective-permute-start | bytes 1327112 | tf_op jit(solution)/shard_map/ppermute | solution.py:316
  10.5 38.6 %collective-permute-start.2 = (f32[4,6,3,1536]{3,0,2,1:T(4,128)}, f32[4,6,3,1536]{3,0,2,1:T(4,128)}, u32[]{:S(2)}, u32[]{:S(2)}) collective-permute-start(f32[4,6,3,1536]{3,0,2,1:T(4,128)} %get-tuple-element.53), channel_id=1, source_target_pairs={{0,1},{1,2},{2,3},{3,4},{4,5},{5,6},{6,7},{7,0},{8,9},{9,10},{10,1... | collective-permute-start | bytes 1327112 | tf_op jit(solution)/shard_map/ppermute | solution.py:316
  13.7 36.7 %copy-start.3 = (f32[4,6,6,1536]{3,2,1,0:T(8,128)}, f32[4,6,6,1536]{3,2,1,0:T(8,128)S(1)}, u32[]{:S(2)}) copy-start(f32[4,6,6,1536]{3,2,1,0:T(8,128)S(1)} %copy.37.v_ref) | copy-start | bytes 2654212
  20.1 1.5 copy-start.50
  20.1 1.6 copy-start.51
  20.1 2.2 %copy-start.42 = (f32[1536]{0:T(1024)S(1)}, f32[1536]{0:T(1024)}, u32[]{:S(2)}) copy-start(f32[1536]{0:T(1024)} %fusion.2) | copy-start | bytes 18436
  20.1 2.2 %copy-start.49 = (f32[6]{0:T(128)S(1)}, f32[6]{0:T(128)}, u32[]{:S(2)}) copy-start(f32[6]{0:T(128)} %sine_multiply_fusion) | copy-start | bytes 76
  21.6 57.1 %copy-start = (s32[4,6,6,1536]{3,2,1,0:T(8,128)}, s32[4,6,6,1536]{3,2,1,0:T(8,128)S(1)}, u32[]{:S(2)}) copy-start(s32[4,6,6,1536]{3,2,1,0:T(8,128)S(1)} %copy.44.obstacle_ref) | copy-start | bytes 2654212
  23.1 27.3 %copy-start.32 = (f32[6,1,1536]{2,1,0:T(1,128)}, f32[6,1,1536]{2,1,0:T(1,128)S(1)}, u32[]{:S(2)}) copy-start(f32[6,1,1536]{2,1,0:T(1,128)S(1)} %multiply_multiply_fusion.2.f2_ref) | copy-start | bytes 110596
  23.1 21.6 %copy-start.48 = (f32[4]{0:T(128)S(1)}, f32[4]{0:T(128)}, u32[]{:S(2)}) copy-start(f32[4]{0:T(128)} %fusion.12) | copy-start | bytes 52
  23.9 22.8 %copy-start.5 = (f32[6,6,1536]{2,1,0:T(8,128)}, f32[6,6,1536]{2,1,0:T(8,128)S(1)}, u32[]{:S(2)}) copy-start(f32[6,6,1536]{2,1,0:T(8,128)S(1)} %multiply_multiply_fusion.1.f0_ref) | copy-start | bytes 663556
  24.6 22.1 %copy-start.8 = (f32[6,6,1536]{2,1,0:T(8,128)}, f32[6,6,1536]{2,1,0:T(8,128)S(1)}, u32[]{:S(2)}) copy-start(f32[6,6,1536]{2,1,0:T(8,128)S(1)} %multiply_multiply_fusion.f4_ref) | copy-start | bytes 663556
  24.7 22.0 %copy-start.29 = (f32[4,6,384]{2,1,0:T(8,128)}, f32[4,6,384]{2,1,0:T(8,128)S(1)}, u32[]{:S(2)}) copy-start(f32[4,6,384]{2,1,0:T(8,128)S(1)} %broadcast_in_dim.14.f3_ref) | copy-start | bytes 110596
  43.0 1.7 copy-start.13
  45.5 4.9 %copy-start.35 = (f32[4,1,1536]{2,1,0:T(1,128)}, f32[4,1,1536]{2,1,0:T(1,128)S(1)}, u32[]{:S(2)}) copy-start(f32[4,1,1536]{2,1,0:T(1,128)S(1)} %multiply_multiply_fusion.3.f1_ref) | copy-start | bytes 73732
  50.4 28.1 %copy-start.45 = (f32[5]{0:T(128)S(1)}, f32[5]{0:T(128)}, u32[]{:S(2)}) copy-start(f32[5]{0:T(128)} %constant.87) | copy-start | bytes 64
  60.9 1.5 copy-start.19
  62.3 1.0 copy-start.25
  63.4 0.6 copy-start.39
  78.7 1.3 copy-start.4
  80.0 2.0 copy-start.14
  82.0 1.7 copy-start.20
  83.6 1.3 copy-start.26
  87.5 7.2 %copy-start.6 = (f32[6,6,1536]{2,1,0:T(8,128)S(1)}, f32[6,6,1536]{2,1,0:T(8,128)}, u32[]{:S(2)}) copy-start(f32[6,6,1536]{2,1,0:T(8,128)} %copy-done.5) | copy-start | bytes 663556
  87.5 7.2 %copy-start.9 = (f32[6,6,1536]{2,1,0:T(8,128)S(1)}, f32[6,6,1536]{2,1,0:T(8,128)}, u32[]{:S(2)}) copy-start(f32[6,6,1536]{2,1,0:T(8,128)} %copy-done.8) | copy-start | bytes 663556
  87.5 7.2 %copy-start.30 = (f32[4,6,384]{2,1,0:T(8,128)S(1)}, f32[4,6,384]{2,1,0:T(8,128)}, u32[]{:S(2)}) copy-start(f32[4,6,384]{2,1,0:T(8,128)} %copy-done.29) | copy-start | bytes 110596
  87.5 27.3 %collective-permute-start.6 = (f32[4,6,3,1536]{3,0,2,1:T(4,128)S(1)}, f32[4,6,3,1536]{3,0,2,1:T(4,128)S(1)}, u32[]{:S(2)}, u32[]{:S(2)}) collective-permute-start(f32[4,6,3,1536]{3,0,2,1:T(4,128)S(1)} %copy.47), channel_id=1, source_target_pairs={{0,1},{1,2},{2,3},{3,4},{4,5},{5,6},{6,7},{7,0},{8,9},{9,10},{10,1... | collective-permute-start | bytes 1327112 | tf_op jit(solution)/shard_map/ppermute | solution.py:316
  87.7 27.3 %collective-permute-start.7 = (f32[4,6,3,1536]{3,0,2,1:T(4,128)S(1)}, f32[4,6,3,1536]{3,0,2,1:T(4,128)S(1)}, u32[]{:S(2)}, u32[]{:S(2)}) collective-permute-start(f32[4,6,3,1536]{3,0,2,1:T(4,128)S(1)} %copy.48), channel_id=1, source_target_pairs={{1,0},{2,1},{3,2},{4,3},{5,4},{6,5},{7,6},{0,7},{9,8},{10,9},{11,1... | collective-permute-start | bytes 1327112 | tf_op jit(solution)/shard_map/ppermute | solution.py:316
  91.4 23.9 %collective-permute-start.4 = (f32[4,3,6,1536]{3,0,2,1:T(4,128)S(1)}, f32[4,3,6,1536]{3,0,2,1:T(4,128)S(1)}, u32[]{:S(2)}, u32[]{:S(2)}) collective-permute-start(f32[4,3,6,1536]{3,0,2,1:T(4,128)S(1)} %copy.45), channel_id=1, source_target_pairs={{0,8},{8,16},{16,24},{24,0},{1,9},{9,17},{17,25},{25,1},{2,10},{10... | collective-permute-start | bytes 1327112 | tf_op jit(solution)/shard_map/ppermute | solution.py:316
  93.1 22.4 %collective-permute-start.5 = (f32[4,3,6,1536]{3,0,2,1:T(4,128)S(1)}, f32[4,3,6,1536]{3,0,2,1:T(4,128)S(1)}, u32[]{:S(2)}, u32[]{:S(2)}) collective-permute-start(f32[4,3,6,1536]{3,0,2,1:T(4,128)S(1)} %copy.46), channel_id=1, source_target_pairs={{8,0},{16,8},{24,16},{0,24},{9,1},{17,9},{25,17},{1,25},{10,2},{18... | collective-permute-start | bytes 1327112 | tf_op jit(solution)/shard_map/ppermute | solution.py:316
  113.1 1.7 copy-start.15
  115.3 0.8 copy-start.33
  115.3 0.8 copy-start.36
  116.1 24.3 %copy-start.46 = (f32[5]{0:T(128)S(1)}, f32[5]{0:T(128)}, u32[]{:S(2)}) copy-start(f32[5]{0:T(128)} %constant.81) | copy-start | bytes 64
  126.5 1.5 copy-start.21
  127.9 1.1 copy-start.27
  129.0 0.6 copy-start.40
  141.7 1.3 copy-start.1
  143.0 2.0 copy-start.16
  145.0 1.7 copy-start.22
  146.7 1.3 copy-start.28
  150.6 7.4 %copy-start.7 = (f32[6,6,1536]{2,1,0:T(8,128)S(1)}, f32[6,6,1536]{2,1,0:T(8,128)}, u32[]{:S(2)}) copy-start(f32[6,6,1536]{2,1,0:T(8,128)} %copy-done.5) | copy-start | bytes 663556
  150.6 7.4 %copy-start.10 = (f32[6,6,1536]{2,1,0:T(8,128)S(1)}, f32[6,6,1536]{2,1,0:T(8,128)}, u32[]{:S(2)}) copy-start(f32[6,6,1536]{2,1,0:T(8,128)} %copy-done.8) | copy-start | bytes 663556
  150.6 7.4 %copy-start.31 = (f32[4,6,384]{2,1,0:T(8,128)S(1)}, f32[4,6,384]{2,1,0:T(8,128)}, u32[]{:S(2)}) copy-start(f32[4,6,384]{2,1,0:T(8,128)} %copy-done.29) | copy-start | bytes 110596
  150.6 27.4 %collective-permute-start.10 = (f32[4,6,3,1536]{3,0,2,1:T(4,128)S(1)}, f32[4,6,3,1536]{3,0,2,1:T(4,128)S(1)}, u32[]{:S(2)}, u32[]{:S(2)}) collective-permute-start(f32[4,6,3,1536]{3,0,2,1:T(4,128)S(1)} %copy.57), channel_id=1, source_target_pairs={{0,1},{1,2},{2,3},{3,4},{4,5},{5,6},{6,7},{7,0},{8,9},{9,10},{10,1... | collective-permute-start | bytes 1327112 | tf_op jit(solution)/shard_map/ppermute | solution.py:316
  150.7 27.5 %collective-permute-start.11 = (f32[4,6,3,1536]{3,0,2,1:T(4,128)S(1)}, f32[4,6,3,1536]{3,0,2,1:T(4,128)S(1)}, u32[]{:S(2)}, u32[]{:S(2)}) collective-permute-start(f32[4,6,3,1536]{3,0,2,1:T(4,128)S(1)} %copy.58), channel_id=1, source_target_pairs={{1,0},{2,1},{3,2},{4,3},{5,4},{6,5},{7,6},{0,7},{9,8},{10,9},{11,1... | collective-permute-start | bytes 1327112 | tf_op jit(solution)/shard_map/ppermute | solution.py:316
  154.5 24.1 %collective-permute-start.8 = (f32[4,3,6,1536]{3,0,2,1:T(4,128)S(1)}, f32[4,3,6,1536]{3,0,2,1:T(4,128)S(1)}, u32[]{:S(2)}, u32[]{:S(2)}) collective-permute-start(f32[4,3,6,1536]{3,0,2,1:T(4,128)S(1)} %copy.55), channel_id=1, source_target_pairs={{0,8},{8,16},{16,24},{24,0},{1,9},{9,17},{17,25},{25,1},{2,10},{10... | collective-permute-start | bytes 1327112 | tf_op jit(solution)/shard_map/ppermute | solution.py:316
  155.9 22.8 %collective-permute-start.9 = (f32[4,3,6,1536]{3,0,2,1:T(4,128)S(1)}, f32[4,3,6,1536]{3,0,2,1:T(4,128)S(1)}, u32[]{:S(2)}, u32[]{:S(2)}) collective-permute-start(f32[4,3,6,1536]{3,0,2,1:T(4,128)S(1)} %copy.56), channel_id=1, source_target_pairs={{8,0},{16,8},{24,16},{0,24},{9,1},{17,9},{25,17},{1,25},{10,2},{18... | collective-permute-start | bytes 1327112 | tf_op jit(solution)/shard_map/ppermute | solution.py:316
  176.3 1.7 copy-start.11
  178.5 0.8 copy-start.34
  178.5 0.8 copy-start.37
  179.3 24.8 %copy-start.47 = (f32[5]{0:T(128)S(1)}, f32[5]{0:T(128)}, u32[]{:S(2)}) copy-start(f32[5]{0:T(128)} %constant.81) | copy-start | bytes 64
  179.3 26.8 %copy-start.2 = (s32[4,6,6,1536]{3,2,1,0:T(8,128)S(1)}, s32[4,6,6,1536]{3,2,1,0:T(8,128)}, u32[]{:S(2)}) copy-start(s32[4,6,6,1536]{3,2,1,0:T(8,128)} %copy-done) | copy-start | bytes 2654212
  189.7 1.5 copy-start.17
  191.2 1.1 copy-start.23
  206.1 2.0 copy-start.12
  208.1 1.7 copy-start.18
  209.8 1.3 copy-start.24
  (1 other events, 0.6 us)
where the time goes:
time: 215 us; the launch traced here: 214 us
  Pallas kernels  123 us (57%)
  local copies, waits for them, and re-layouts  53.9 us (25%)
  starting transfers between devices  20.1 us (9%)
  other arithmetic  9.95 us (5%)
  between operations  6.76 us (3%)
    pallas_call x9, Pallas kernels, call(): pl.pallas_call(kernel, out_shape=[jax.ShapeDtypeStruct(s, jnp.float32) fo...  91.2 us
    unnamed x110, local copies, waits for them, and re-layouts  37.6 us
    pallas_call x3, Pallas kernels, peak_everywhere(): pl.pallas_call(functools.partial(peak_kernel, sizes), out_shape=jax.Shape...  32.3 us
    ppermute x12, starting transfers between devices, exchange(): return (lax.ppermute(part_hi, axis, up), lax.ppermute(part_lo, axis, down))  20.1 us
    ppermute x12, local copies, waits for them, and re-layouts, exchange(): return (lax.ppermute(part_hi, axis, up), lax.ppermute(part_lo, axis, down))  6.34 us
  transfers between devices with their start and end apart: 12, of which 0 were waited for; matrix products, arithmetic and copies ran while one was open for 9% of the time, Pallas kernels for 26%

commit v1 on v0

v1 whole, which is shorter than its diff:
```python
import functools
import math

import jax
import jax.numpy as jnp
import numpy as np
from jax import lax
from jax.experimental import pallas as pl
from jax.experimental.pallas import tpu as pltpu
from jax.sharding import PartitionSpec as P

N3 = 32
N4 = 48
GRID = 96
STEPS = 3
COURANT = 0.5
EPS = 0.75e-6
LANES = 128
PAD = 16
MESH = pl.DeviceIdType.MESH


def sub(x, y):
    if x is None or y is None:
        return x if y is None else -y
    return x - y


def add(x, y):
    if x is None or y is None:
        return x if y is None else y
    return x + y


def mul(x, y):
    return None if x is None or y is None else x * y


def wave(d):
    n = len(d) - 5
    f = [sub(d[k + 1], d[k]) for k in range(n + 4)]
    e = [sub(f[k + 1], f[k]) for k in range(n + 3)]
    j = [sub(e[k + 1], e[k]) for k in range(n + 2)]
    g = [mul(0.75, x) for x in f]
    g2 = [add(x, x) for x in g]
    base = [add(add(mul(e[k], e[k]), EPS), mul(g[k], f[k + 1])) for k in range(n + 3)]
    left, mid, right = [], [], []
    for k in range(n + 1):
        a = add(base[k], mul(g2[k + 1], e[k]))
        b = base[k + 1]
        c = sub(base[k + 2], mul(g2[k + 2], e[k + 2]))
        left.append(a * a)
        mid.append(b * b)
        right.append(c * c)
    low, high = [], []
    for k in range(n + 1):
        bc = mid[k] * right[k]
        ab = left[k] * mid[k]
        ac = 6.0 * (left[k] * right[k])
        n1 = mul(bc, j[k])
        n2 = mul(ab, j[k + 1])
        if 0 < k < n:
            both = add(n1, n2)
            both = add(both, both)
            core = (bc + ab) + ac
            low.append(add(both, n2) / (core + (ab + ab)))
            high.append(add(both, n1) / (core + (bc + bc)))
        elif k == 0:
            low.append(add(add(n1, n1), 3.0 * n2) / ((bc + ac) + 3.0 * ab))
            high.append(None)
        else:
            low.append(None)
            high.append(add(add(n2, n2), mul(3.0, n1)) / ((ab + ac) + 3.0 * bc))
    out = []
    for i in range(n):
        rm, rp = low[i], high[i + 1]
        center = mul(6.0, add(d[i + 3], d[i + 2]))
        middle = add(sub(center, add(e[i + 1], e[i + 2])), rp - rm)
        jump = sub(rp + rm, j[i + 1])
        out.append((middle, jump))
    return out


def gaps(vs):
    return [None if a is b else b - a for a, b in zip(vs[:-1], vs[1:])]


def tally(middle, jump, drift, kappa):
    gap = drift - middle
    return jnp.abs(gap) + jnp.abs(jump), (kappa * middle) * (drift + gap)


def kernel(
    dims, sizes,
    cost_ref, gain_ref, trig_ref, v_hbm, t_hbm, o_hbm,
    out_hbm, dt_ref,
    v, t, o, h, q, ra, rb, ca, cb, f0, f1, f2, f3, f4r, f4k, keep, own, slots,
    in_sem, out_sem, rs_sem, rr_sem, cs_sem, cr_sem, ts_sem, tr_sem,
):
    planes, rows, cols, width = dims
    nx, ny = sizes
    chunks = width // LANES
    block = planes * chunks
    parts = block // 8
    pair = 8 // planes
    cells = rows * cols
    ix, iy = lax.axis_index("gx"), lax.axis_index("gy")
    n = nx * ny
    me = ix * ny + iy
    h1 = 2.0 * math.pi / (rows * nx)
    h2 = 2.0 * math.pi / (cols * ny)
    spacing = [2.0 / GRID, h1, h2, 2.0 / GRID, 2.0 / GRID]

    def place(k):
        other = (me + k) % n
        return (other // ny, other % ny)

    def at(c, r):
        return PAD + (c * rows + r) * block

    def span(start, size=8):
        return pl.ds(pl.multiple_of(start, 8), size)

    def loads(c):
        out = []
        for r in range(rows):
            out.append(
                pltpu.make_async_copy(
                    v_hbm.at[r * cols + c],
                    v.at[pl.ds(PAD + (c * rows + r) * block, block)],
                    in_sem.at[c * rows + r],
                )
            )
        return out

    def masks():
        out = []
        for slot, (src, dst) in enumerate(((t_hbm, t), (o_hbm, o))):
            for c in range(cols):
                for r in range(rows):
                    out.append(
                        pltpu.make_async_copy(
                            src.at[r * cols + c],
                            dst.at[pl.ds((c * rows + r) * block, block)],
                            in_sem.at[(slot + 1) * cells + c * rows + r],
                        )
                    )
        return out

    def stores(c):
        out = []
        for r in range(rows):
            out.append(
                pltpu.make_async_copy(
                    v.at[pl.ds(PAD + (c * rows + r) * block, block)],
                    out_hbm.at[r * cols + c],
                    out_sem.at[c * rows + r],
                )
            )
        return out

    tall = 3 * block
    up = ((ix + 1) % nx, iy)
    down = ((ix + nx - 1) % nx, iy)
    after = (ix, (iy + 1) % ny)
    before = (ix, (iy + ny - 1) % ny)

    def row_copy(c, which):
        first = PAD + c * rows * block + (0 if which else (rows - 3) * block)
        return pltpu.make_async_remote_copy(
            src_ref=v.at[pl.ds(first, tall)],
            dst_ref=(rb if which else ra).at[pl.ds(c * tall, tall)],
            send_sem=rs_sem.at[c, which],
            recv_sem=rr_sem.at[c, which],
            device_id=down if which else up,
            device_id_type=MESH,
        )

    def col_copy(c, which):
        wide = rows * block
        i = c if which else c - (cols - 3)
        return pltpu.make_async_remote_copy(
            src_ref=v.at[pl.ds(PAD + c * wide, wide)],
            dst_ref=(cb if which else ca).at[pl.ds(i * wide, wide)],
            send_sem=cs_sem.at[i, which],
            recv_sem=cr_sem.at[i, which],
            device_id=before if which else after,
            device_id_type=MESH,
        )

    def col_copies(c):
        out = []
        if c < 3:
            out.append(col_copy(c, 1))
        if c >= cols - 3:
            out.append(col_copy(c, 0))
        return out

    def sends(c):
        return [row_copy(c, 0), row_copy(c, 1)] + col_copies(c)

    for c in range(cols):
        for copy in loads(c):
            copy.start()
    for copy in masks():
        copy.start()

    barrier = pltpu.get_barrier_semaphore()

    def greet(k, carry):
        pl.semaphore_signal(barrier, inc=1, device_id=place(k), device_id_type=MESH)
        return carry

    lax.fori_loop(1, n, greet, 0)

    full = lambda x: jnp.full((8, LANES), x, jnp.float32)
    kappa = [full(cost_ref[i]) * (1.0 / (288.0 * spacing[i])) for i in range(5)]
    gain = [full(gain_ref[i]) * 12.0 / full(cost_ref[i]) for i in range(5)]
    base_b = 2 * rows * nx
    cos_a = lambda r: full(trig_ref[ix * rows + r])
    sin_a = lambda r: full(trig_ref[rows * nx + ix * rows + r])
    cos_b = lambda c: full(trig_ref[base_b + iy * cols + c])
    sin_b = lambda c: full(trig_ref[base_b + cols * ny + iy * cols + c])

    lane = lax.broadcasted_iota(jnp.int32, (8, LANES), 1)
    sublane = lax.broadcasted_iota(jnp.int32, (8, LANES), 0)
    x0 = ((sublane % planes).astype(jnp.float32) - planes / 2 + 0.5) * (2.0 / GRID)
    v[0:PAD, :] = jnp.zeros((PAD, LANES), jnp.float32)
    v[PAD + cells * block :, :] = jnp.zeros((PAD, LANES), jnp.float32)
    for k in range(parts):
        index = (k * pair + sublane // planes) * LANES + lane
        third, fourth = index // N4, index % N4
        x3 = (third.astype(jnp.float32) - N3 / 2 + 0.5) * (2.0 / GRID)
        x4 = (fourth.astype(jnp.float32) - N4 / 2 + 0.5) * (2.0 / GRID)
        f1[8 * k : 8 * k + 8, :] = gain[1] * (x4 - 0.3 * x0)
        f4k[8 * k : 8 * k + 8, :] = gain[4] * x4
        for r in range(rows):
            f2[8 * (r * parts + k) : 8 * (r * parts + k) + 8, :] = gain[2] * (x3 + 0.5 * sin_a(r))
        for slot, (spot, extent) in enumerate(((third, width // N4), (fourth, N4))):
            for i, off in enumerate((-3, -2, -1, 1, 2, 3)):
                good = (spot + off >= 0) & (spot + off < extent)
                first = 8 * ((slot * parts + k) * 6 + i)
                keep[first : first + 8, :] = jnp.where(good, 1.0, 0.0)
    for c in range(cols):
        f3[8 * c : 8 * c + 8, :] = gain[3] * (sin_b(c) - x0)
        for r in range(rows):
            i = c * rows + r
            f4r[8 * i : 8 * i + 8, :] = gain[4] * (cos_a(r) * sin_b(c))
    rowid = lax.broadcasted_iota(jnp.int32, (chunks, LANES), 0)
    laneid = lax.broadcasted_iota(jnp.int32, (chunks, LANES), 1)
    x3 = (((rowid * LANES + laneid) // N4).astype(jnp.float32) - N3 / 2 + 0.5) * (2.0 / GRID)
    for c in range(cols):
        for r in range(rows):
            i = c * rows + r
            bias = cos_a(r) - 0.5 * cos_b(c)
            f0[i * chunks : (i + 1) * chunks, :] = gain[0][0:1] * (bias[0:1] + x3)

    pl.semaphore_wait(barrier, n - 1)
    for c in range(cols):
        for copy in loads(c):
            copy.wait()
        for copy in sends(c):
            copy.start()

    zero = jnp.zeros((8, LANES), jnp.float32)

    def along_planes(g, top):
        def spot(p):
            return pl.ds(g * 8 * planes + p, 8, stride=planes)

        vs = [v[pl.ds(PAD + g * 8 * planes + p, 8, stride=planes), :] for p in range(planes)]
        drift = f0[span(g * 8), :]
        cellsp = wave(gaps([vs[0]] * 3 + vs + [vs[-1]] * 3))
        for p in range(planes):
            speed, part = tally(*cellsp[p], drift, kappa[0])
            top = jnp.maximum(top, speed)
            h[spot(p), :] = part
            q[0, spot(p), :] = cellsp[p][1]
        return top

    def along_lanes(slot, k, stride):
        number = 3 + slot

        def near(first, off):
            return v[pl.ds(first + off * planes, 8), :]

        def one(i, top):
            first = PAD + i * block + 8 * k
            vs = []
            for s in (-3, -2, -1, 0, 1, 2, 3):
                if s == 0:
                    vs.append(near(first, 0))
                    continue
                whole, rest = divmod(abs(s) * stride, LANES)
                if s > 0:
                    x = jnp.where(lane < rest, near(first, whole + 1), near(first, whole))
                    vs.append(pltpu.roll(x, LANES - rest, 1))
                else:
                    x = jnp.where(lane >= LANES - rest, near(first, -whole - 1), near(first, -whole))
                    vs.append(pltpu.roll(x, rest, 1))
            d = []
            for b in range(6):
                x = vs[b + 1] - vs[b]
                edge = slot == 1 or (k == 0 and b < 3) or (k == parts - 1 and b >= 3)
                if edge:
                    row = 8 * ((slot * parts + k) * 6 + b)
                    x = x * keep[row : row + 8, :]
                d.append(x)
            ((middle, jump),) = wave(d)
            if slot:
                drift = f4r[span(i * 8), :] - f4k[8 * k : 8 * k + 8, :]
            else:
                drift = f3[span(i // rows * 8), :]
            speed, part = tally(middle, jump, drift, kappa[number])
            here = span(i * block + 8 * k)
            q[number, here, :] = jump
            h[here, :] = h[here, :] + part
            return jnp.maximum(top, speed)

        def some(i, top):
            for u in range(3):
                top = one(i * 3 + u, top)
            return top

        return some

    def along_cols(i, top):
        r, k = i // parts, i % parts
        rim = [span((m * rows + r) * block + 8 * k) for m in range(3)]
        vs = [ca[x, :] for x in rim]
        vs += [v[span(PAD + (c * rows + r) * block + 8 * k), :] for c in range(cols)]
        vs += [cb[x, :] for x in rim]
        drift = f2[span(i * 8), :]
        for c, (middle, jump) in enumerate(wave(gaps(vs))):
            speed, part = tally(middle, jump, drift, kappa[2])
            top = jnp.maximum(top, speed)
            here = span((c * rows + r) * block + 8 * k)
            h[here, :] = h[here, :] + part
            q[2, here, :] = jump
        return top

    def along_rows(c, k, top):
        rim = [span((c * 3 + m) * block + 8 * k) for m in range(3)]
        vs = [ra[x, :] for x in rim]
        vs += [v[span(PAD + (c * rows + r) * block + 8 * k), :] for r in range(rows)]
        vs += [rb[x, :] for x in rim]
        drift = f1[span(k * 8), :]
        for r, (middle, jump) in enumerate(wave(gaps(vs))):
            speed, part = tally(middle, jump, drift, kappa[1])
            top = jnp.maximum(top, speed)
            here = span((c * rows + r) * block + 8 * k)
            h[here, :] = h[here, :] + part
            q[1, here, :] = jump
        return top

    def step(s, carry):
        tops = [None] * 5
        tops[0] = lax.fori_loop(0, cells * block // (8 * planes), along_planes, zero)
        for slot, stride in ((0, N4), (1, 1)):
            top = zero
            for k in range(parts):
                top = lax.fori_loop(0, cells // 3, along_lanes(slot, k, stride), top)
            tops[3 + slot] = top
        for c in range(3):
            for which in range(2):
                col_copy(c if which else c + cols - 3, which).wait()
        tops[2] = lax.fori_loop(0, rows * parts, along_cols, zero)
        row = lax.broadcasted_iota(jnp.int32, (8, LANES), 0)
        early = zero
        for number in (0, 2, 3, 4):
            early = jnp.where(row == number, jnp.max(tops[number]), early)
        top = zero
        for c in range(cols):
            for which in range(2):
                row_copy(c, which).wait()
            top = lax.fori_loop(0, parts, functools.partial(along_rows, c), top)
        own[...] = jnp.where(row == 1, jnp.max(top), early)

        def peak_copy(k):
            return pltpu.make_async_remote_copy(
                src_ref=own,
                dst_ref=slots.at[s, k],
                send_sem=ts_sem.at[k],
                recv_sem=tr_sem.at[s, k],
                device_id=place(k),
                device_id_type=MESH,
            )

        def send(k, carry):
            peak_copy(k).start()
            return carry

        def take(k, best):
            peak_copy(k).wait_recv()
            return jnp.maximum(best, slots[s, k])

        def finish(k, carry):
            peak_copy(k).wait_send()
            return carry

        lax.fori_loop(1, n, send, 0)
        best = lax.fori_loop(1, n, take, own[...])
        lax.fori_loop(1, n, finish, 0)
        spread = lambda i: jnp.broadcast_to(best[i : i + 1, :], (8, LANES))
        bounds = [spread(i) * full(cost_ref[i]) * (1.0 / 12.0) for i in range(5)]
        total = bounds[0] * (1.0 / spacing[0])
        for i in range(1, 5):
            total = total + bounds[i] * (1.0 / spacing[i])
        dt = COURANT / (total + 1e-6)
        scale = [dt * bounds[i] * (1.0 / (12.0 * spacing[i])) for i in range(5)]
        dt_ref[s] = dt[0, 0]

        @pl.when(s == 0)
        def _():
            for copy in masks():
                copy.wait()

        for c in range(cols):
            def move(i, carry):
                row = c * rows * block + i * 8
                here = span(row)
                change = dt * h[here, :]
                for number in range(5):
                    change = change - scale[number] * q[number, here, :]
                new = v[span(PAD + row), :] - change
                new = jnp.where(t[here, :] == 1, jnp.minimum(new, -0.5), new)
                v[span(PAD + row), :] = jnp.where(o[here, :] == 1, jnp.maximum(new, 0.5), new)
                return carry

            lax.fori_loop(0, rows * parts, move, 0, unroll=4)

            @pl.when(s < STEPS - 1)
            def _():
                for copy in sends(c):
                    copy.start()

            @pl.when(s == STEPS - 1)
            def _():
                for copy in stores(c):
                    copy.start()

        return carry

    lax.fori_loop(0, STEPS, step, 0)
    for c in range(cols):
        for copy in stores(c):
            copy.wait()


VMEM = pl.BlockSpec(memory_space=pltpu.VMEM)
SMEM = pl.BlockSpec(memory_space=pltpu.SMEM)
ANY = pl.BlockSpec(memory_space=pl.ANY)


def fold(x):
    planes, rows, cols, width = x.shape
    chunks = width // LANES
    x = x.reshape(planes, rows, cols, chunks, LANES).transpose(1, 2, 3, 0, 4)
    return x.reshape(rows * cols, chunks * planes, LANES)


def unfold(x, shape):
    planes, rows, cols, width = shape
    x = x.reshape(rows, cols, width // LANES, planes, LANES).transpose(3, 0, 1, 2, 4)
    return x.reshape(shape)


def body(value, target, obstacle, gains, costs):
    dims = value.shape
    planes, rows, cols, width = dims
    nx, ny = lax.axis_size("gx"), lax.axis_size("gy")
    block = planes * width // LANES
    parts = block // 8
    cells = rows * cols
    whole = cells * block
    one = np.float32(2.0 * math.pi / (rows * nx)) * np.arange(rows * nx, dtype=np.float32)
    two = np.float32(2.0 * math.pi / (cols * ny)) * np.arange(cols * ny, dtype=np.float32)
    one, two = one.astype(np.float64), two.astype(np.float64)
    trig = np.concatenate([np.cos(one), np.sin(one), np.cos(two), np.sin(two)])
    trig = jnp.asarray(trig.astype(np.float32))
    f32 = lambda *shape: pltpu.VMEM(shape, jnp.float32)
    i32 = lambda *shape: pltpu.VMEM(shape, jnp.int32)
    dma = lambda *shape: pltpu.SemaphoreType.DMA(shape)
    n = nx * ny
    out, steps = pl.pallas_call(
        functools.partial(kernel, dims, (nx, ny)),
        out_shape=[
            jax.ShapeDtypeStruct((cells, block, LANES), jnp.float32),
            jax.ShapeDtypeStruct((STEPS,), jnp.float32),
        ],
        in_specs=[SMEM, SMEM, SMEM, ANY, ANY, ANY],
        out_specs=[ANY, SMEM],
        scratch_shapes=[
            f32(whole + 2 * PAD, LANES), i32(whole, LANES), i32(whole, LANES),
            f32(whole, LANES), f32(5, whole, LANES),
            f32(cols * 3 * block, LANES), f32(cols * 3 * block, LANES),
            f32(rows * 3 * block, LANES), f32(rows * 3 * block, LANES),
            f32(whole // planes, LANES), f32(8 * parts, LANES), f32(8 * rows * parts, LANES),
            f32(8 * cols, LANES), f32(8 * cells, LANES), f32(8 * parts, LANES),
            f32(8 * 12 * parts, LANES), f32(8, LANES), f32(STEPS, n, 8, LANES),
            dma(3 * cells), dma(cells), dma(cols, 2), dma(cols, 2), dma(3, 2), dma(3, 2),
            dma(n), dma(STEPS, n),
        ],
        compiler_params=pltpu.CompilerParams(
            collective_id=0, has_side_effects=True, vmem_limit_bytes=40 << 20
        ),
    )(costs, gains, trig, fold(value), fold(target), fold(obstacle))
    return unfold(out, dims), steps


def solution(mesh):
    spec = P(None, "gx", "gy", None)
    return jax.shard_map(
        body,
        mesh=mesh,
        in_specs=(spec, spec, spec, P(), P()),
        out_specs=(spec, P()),
        check_vma=False,
    )
```

time: 215 us -> 120 us (0.56)
  local copies, waits for them, and re-layouts: 53.9 us -> 8.13 us
  starting transfers between devices: 20.1 us -> 0 us
  Pallas kernels: 123 us -> 111 us
  other arithmetic: 9.95 us -> 0 us
  between operations: 6.76 us -> 0.7 us
    unnamed x110 -> x7, local copies, waits for them, and re-layouts: 37.6 us -> 0.8 us
    ppermute x12 -> x0, starting transfers between devices: 20.1 us -> none  [exchange(): return (lax.ppermute(part_hi, axis, up), lax.ppermute(part_lo, axis, down))]
    pallas_call x12 -> x1, Pallas kernels: 123 us -> 111 us  [body(): pl.pallas_call(functools.partial(kernel, dims, (nx, ny)), out_shape=[jax....]
    slice x19 -> x0, local copies, waits for them, and re-layouts: 9.94 us -> none  [the longest x7 3.5 us: body(): a_lo, a_hi = exchange(value[:, :3], value[:, -3:], 'gx')]
    ppermute x12 -> x0, local copies, waits for them, and re-layouts: 6.34 us -> none  [exchange(): return (lax.ppermute(part_hi, axis, up), lax.ppermute(part_lo, axis, down))]
    reshape x0 -> x5, local copies, waits for them, and re-layouts: none -> 6.22 us  [the longest x3 4.87 us: fold(): x = x.reshape(planes, rows, cols, chunks, LANES).transpose(1, 2, 3, 0, 4)]
    mul x12 -> x0, other arithmetic: 6.09 us -> none  [the longest x5 3.62 us: body(): f = [d * (12.0 / costs[i]) for i, d in enumerate(drifts(shape, gains))]]
    reduce_sum x3 -> x0, other arithmetic: 2.47 us -> none  [body(): dt = COURANT / (jnp.sum(bounds / h) + 1e-06)]
  transfers between devices with their start and end apart: 12 -> 0, of which waited for: 0 -> 0; matrix products, arithmetic and copies ran while one was open for 9% -> 0% of each run, Pallas kernels for 26% -> 0%
where the time goes in v1:
time: 120 us
  Pallas kernels  111 us (92%)
  local copies, waits for them, and re-layouts  8.13 us (7%)
    pallas_call x1, Pallas kernels, body(): pl.pallas_call(functools.partial(kernel, dims, (nx, ny)), out_shape=[jax....  111 us
    reshape x3, local copies, waits for them, and re-layouts, fold(): x = x.reshape(planes, rows, cols, chunks, LANES).transpose(1, 2, 3, 0, 4)  4.87 us

profile of v1, /device:TPU:0, one launch (start us, length us, event | category | flops | bytes accessed | tf_op | source)
XLA Modules:
  0.0 119.8 jit_solution(13584742034473100874)
XLA Ops:
  0.6 1.6 %reshape.28 = f32[4,6,6,12,128]{4,3,0,2,1:T(8,128)S(1)} reshape(f32[4,6,6,1536]{3,0,2,1:T(4,128)} %param.6) | data formatting | bytes 1769472 | tf_op jit(solution)/shard_map/reshape | solution.py:458
  2.3 0.4 copy.12
  2.6 1.6 %reshape.30 = s32[4,6,6,12,128]{4,3,0,2,1:T(8,128)S(1)} reshape(s32[4,6,6,1536]{3,0,2,1:T(4,128)} %param.7) | data formatting | bytes 1769472 | tf_op jit(solution)/shard_map/reshape | solution.py:458
  4.3 0.4 copy.13
  4.6 1.6 %reshape.32 = s32[4,6,6,12,128]{4,3,0,2,1:T(8,128)S(1)} reshape(s32[4,6,6,1536]{3,0,2,1:T(4,128)} %param.8) | data formatting | bytes 1769472 | tf_op jit(solution)/shard_map/reshape | solution.py:458
  6.3 0.0 copy-start
  6.3 0.0 copy-start.1
  6.3 0.0 copy-start.2
  6.3 0.4 copy.14
  6.7 0.3 copy-done
  7.0 0.0 copy-done.1
  7.0 0.0 copy-done.2
  7.0 110.9 %shard_map.77 = (f32[36,48,128]{2,1,0:T(8,128)S(1)}, f32[3]{0:T(128)S(1)}) custom-call(f32[5]{0:T(128)S(1)} %copy-done.1, f32[5]{0:T(128)S(1)} %copy-done.2, f32[144]{0:T(256)S(1)} %copy-done, f32[36,48,128]{2,1,0:T(8,128)S(1)} %bitcast.18, s32[36,48,128]{2,1,0:T(8,128)S(1)} %bitcast.19, s32[36,48,128]{2,1,0:T(8,128)S(1)} %bitcast.20), custom_call_target="tpu_custom_call" | custom-call | tf_op jit(solution)/shard_map/pallas_call | solution.py:485
  117.9 0.1 copy.17
  118.0 1.2 %reshape.35 = f32[4,6,6,1536]{3,0,2,1:T(4,128)} reshape(f32[4,6,6,12,128]{4,3,0,2,1:T(8,128)S(1)} %bitcast.22) | data formatting | bytes 1769472 | tf_op jit(solution)/shard_map/reshape | solution.py:465
  119.3 0.5 copy.19
Async XLA Ops:
  6.3 0.7 copy-start
  6.3 0.7 copy-start.1
  6.3 0.7 copy-start.2

commit v2 on v1

--- a/solution.py
+++ b/solution.py
@@ -5,6 +5,7 @@
 import jax.numpy as jnp
 import numpy as np
 from jax import lax
+from jax.experimental.layout import Layout, with_layout_constraint
 from jax.experimental import pallas as pl
 from jax.experimental.pallas import tpu as pltpu
 from jax.sharding import PartitionSpec as P
@@ -17,7 +18,9 @@
 EPS = 0.75e-6
 LANES = 128
 PAD = 16
+UNROLL = 3
 MESH = pl.DeviceIdType.MESH
+DENSE = Layout(major_to_minor=(1, 2, 3, 0, 4))
 
 
 def sub(x, y):
@@ -92,10 +95,11 @@
 
 def kernel(
     dims, sizes,
-    cost_ref, gain_ref, trig_ref, v_hbm, t_hbm, o_hbm,
-    out_hbm, dt_ref,
-    v, t, o, h, q, ra, rb, ca, cb, f0, f1, f2, f3, f4r, f4k, keep, own, slots,
-    in_sem, out_sem, rs_sem, rr_sem, cs_sem, cr_sem, ts_sem, tr_sem,
+    cost_hbm, gain_hbm, trig_hbm, v_hbm, t_hbm, o_hbm,
+    out, dt_ref,
+    v, t, o, h, q, ra, rb, ca, cb, f0, f1, f2, f3, f4r, f4k, keep, buf0, buf1, own, slots,
+    in_sem, rs_sem, rr_sem, cs_sem, cr_sem, ts_sem, tr_sem, news,
+    cost_ref, gain_ref, trig_ref, small_sem,
 ):
     planes, rows, cols, width = dims
     nx, ny = sizes
@@ -104,19 +108,12 @@
     parts = block // 8
     pair = 8 // planes
     cells = rows * cols
+    groups = cells // UNROLL
     ix, iy = lax.axis_index("gx"), lax.axis_index("gy")
     n = nx * ny
-    me = ix * ny + iy
     h1 = 2.0 * math.pi / (rows * nx)
     h2 = 2.0 * math.pi / (cols * ny)
     spacing = [2.0 / GRID, h1, h2, 2.0 / GRID, 2.0 / GRID]
-
-    def place(k):
-        other = (me + k) % n
-        return (other // ny, other % ny)
-
-    def at(c, r):
-        return PAD + (c * rows + r) * block
 
     def span(start, size=8):
         return pl.ds(pl.multiple_of(start, 8), size)
@@ -147,18 +144,6 @@
                     )
         return out
 
-    def stores(c):
-        out = []
-        for r in range(rows):
-            out.append(
-                pltpu.make_async_copy(
-                    v.at[pl.ds(PAD + (c * rows + r) * block, block)],
-                    out_hbm.at[r * cols + c],
-                    out_sem.at[c * rows + r],
-                )
-            )
-        return out
-
     tall = 3 * block
     up = ((ix + 1) % nx, iy)
     down = ((ix + nx - 1) % nx, iy)
@@ -199,19 +184,33 @@
     def sends(c):
         return [row_copy(c, 0), row_copy(c, 1)] + col_copies(c)
 
+    around = (up, down, after, before)
+    barrier = pltpu.get_barrier_semaphore()
+    for other in around:
+        pl.semaphore_signal(barrier, inc=1, device_id=other, device_id_type=MESH)
     for c in range(cols):
         for copy in loads(c):
             copy.start()
+
+    smalls = [
+        pltpu.make_async_copy(src, dst, small_sem.at[i])
+        for i, (src, dst) in enumerate(
+            ((cost_hbm, cost_ref), (gain_hbm, gain_ref), (trig_hbm, trig_ref))
+        )
+    ]
+    for copy in smalls:
+        copy.start()
+    pl.semaphore_wait(barrier, 4)
+    for c in range(cols):
+        for copy in loads(c):
+            copy.wait()
+        for copy in sends(c):
+            copy.start()
     for copy in masks():
         copy.start()
 
-    barrier = pltpu.get_barrier_semaphore()
-
-    def greet(k, carry):
-        pl.semaphore_signal(barrier, inc=1, device_id=place(k), device_id_type=MESH)
-        return carry
-
-    lax.fori_loop(1, n, greet, 0)
+    for copy in smalls:
+        copy.wait()
 
     full = lambda x: jnp.full((8, LANES), x, jnp.float32)
     kappa = [full(cost_ref[i]) * (1.0 / (288.0 * spacing[i])) for i in range(5)]
@@ -242,10 +241,10 @@
                 first = 8 * ((slot * parts + k) * 6 + i)
                 keep[first : first + 8, :] = jnp.where(good, 1.0, 0.0)
     for c in range(cols):
-        f3[8 * c : 8 * c + 8, :] = gain[3] * (sin_b(c) - x0)
         for r in range(rows):
             i = c * rows + r
             f4r[8 * i : 8 * i + 8, :] = gain[4] * (cos_a(r) * sin_b(c))
+            f3[8 * i : 8 * i + 8, :] = gain[3] * (sin_b(c) - x0)
     rowid = lax.broadcasted_iota(jnp.int32, (chunks, LANES), 0)
     laneid = lax.broadcasted_iota(jnp.int32, (chunks, LANES), 1)
     x3 = (((rowid * LANES + laneid) // N4).astype(jnp.float32) - N3 / 2 + 0.5) * (2.0 / GRID)
@@ -254,13 +253,6 @@
             i = c * rows + r
             bias = cos_a(r) - 0.5 * cos_b(c)
             f0[i * chunks : (i + 1) * chunks, :] = gain[0][0:1] * (bias[0:1] + x3)
-
-    pl.semaphore_wait(barrier, n - 1)
-    for c in range(cols):
-        for copy in loads(c):
-            copy.wait()
-        for copy in sends(c):
-            copy.start()
 
     zero = jnp.zeros((8, LANES), jnp.float32)
 
@@ -284,20 +276,23 @@
         def near(first, off):
             return v[pl.ds(first + off * planes, 8), :]
 
-        def one(i, top):
-            first = PAD + i * block + 8 * k
-            vs = []
-            for s in (-3, -2, -1, 0, 1, 2, 3):
-                if s == 0:
-                    vs.append(near(first, 0))
-                    continue
-                whole, rest = divmod(abs(s) * stride, LANES)
-                if s > 0:
-                    x = jnp.where(lane < rest, near(first, whole + 1), near(first, whole))
-                    vs.append(pltpu.roll(x, LANES - rest, 1))
-                else:
-                    x = jnp.where(lane >= LANES - rest, near(first, -whole - 1), near(first, -whole))
-                    vs.append(pltpu.roll(x, rest, 1))
+        def spin(group, buf):
+            for u in range(UNROLL):
+                first = PAD + (group * UNROLL + u) * block + 8 * k
+                for b, s in enumerate((-3, -2, -1, 1, 2, 3)):
+                    whole, rest = divmod(abs(s) * stride, LANES)
+                    if s > 0:
+                        x = jnp.where(lane < rest, near(first, whole + 1), near(first, whole))
+                        x = pltpu.roll(x, LANES - rest, 1)
+                    else:
+                        x = jnp.where(lane >= LANES - rest, near(first, -whole - 1), near(first, -whole))
+                        x = pltpu.roll(x, rest, 1)
+                    row = 8 * (u * 6 + b)
+                    buf[row : row + 8, :] = x
+
+        def one(i, u, buf, top):
+            turned = [buf[8 * (u * 6 + b) : 8 * (u * 6 + b) + 8, :] for b in range(6)]
+            vs = turned[:3] + [near(PAD + i * block + 8 * k, 0)] + turned[3:]
             d = []
             for b in range(6):
                 x = vs[b + 1] - vs[b]
@@ -310,7 +305,7 @@
             if slot:
                 drift = f4r[span(i * 8), :] - f4k[8 * k : 8 * k + 8, :]
             else:
-                drift = f3[span(i // rows * 8), :]
+                drift = f3[span(i * 8), :]
             speed, part = tally(middle, jump, drift, kappa[number])
             here = span(i * block + 8 * k)
             q[number, here, :] = jump
@@ -318,11 +313,19 @@
             return jnp.maximum(top, speed)
 
         def some(i, top):
-            for u in range(3):
-                top = one(i * 3 + u, top)
+            spin(2 * i + 1, buf1)
+            for u in range(UNROLL):
+                top = one(2 * i * UNROLL + u, u, buf0, top)
+            spin((2 * i + 2) % groups, buf0)
+            for u in range(UNROLL):
+                top = one((2 * i + 1) * UNROLL + u, u, buf1, top)
             return top
 
-        return some
+        def run(top):
+            spin(0, buf0)
+            return lax.fori_loop(0, groups // 2, some, top)
+
+        return run
 
     def along_cols(i, top):
         r, k = i // parts, i % parts
@@ -353,55 +356,70 @@
             q[1, here, :] = jump
         return top
 
+    hops = [(after, before)] * (ny // 2 - 1) + [(up, down)] * (nx // 2)
+
+    def tell(i):
+        for other in hops[i]:
+            pl.semaphore_signal(news.at[i], inc=1, device_id=other, device_id_type=MESH)
+
+    def gossip(s, turn):
+        each = -(-len(hops) // (2 * parts))
+        todo = range(turn * each, min((turn + 1) * each, len(hops)))
+
+        @pl.when(s == 0)
+        def _():
+            for i in todo:
+                pl.semaphore_wait(news.at[i], 2)
+                if i + 1 < len(hops):
+                    tell(i + 1)
+
+    tell(0)
+
     def step(s, carry):
         tops = [None] * 5
         tops[0] = lax.fori_loop(0, cells * block // (8 * planes), along_planes, zero)
         for slot, stride in ((0, N4), (1, 1)):
             top = zero
             for k in range(parts):
-                top = lax.fori_loop(0, cells // 3, along_lanes(slot, k, stride), top)
+                top = along_lanes(slot, k, stride)(top)
+                gossip(s, slot * parts + k)
             tops[3 + slot] = top
         for c in range(3):
             for which in range(2):
                 col_copy(c if which else c + cols - 3, which).wait()
         tops[2] = lax.fori_loop(0, rows * parts, along_cols, zero)
-        row = lax.broadcasted_iota(jnp.int32, (8, LANES), 0)
         early = zero
         for number in (0, 2, 3, 4):
-            early = jnp.where(row == number, jnp.max(tops[number]), early)
+            early = jnp.where(lane == number, jnp.max(tops[number]), early)
         top = zero
         for c in range(cols):
             for which in range(2):
                 row_copy(c, which).wait()
             top = lax.fori_loop(0, parts, functools.partial(along_rows, c), top)
-        own[...] = jnp.where(row == 1, jnp.max(top), early)
+        mine = jnp.where(lane == 1, jnp.max(top), early)
+        own[...] = mine
 
         def peak_copy(k):
+            other = ((ix + k // ny) % nx, (iy + k % ny) % ny)
             return pltpu.make_async_remote_copy(
-                src_ref=own,
-                dst_ref=slots.at[s, k],
+                src_ref=own.at[pl.ds(0, 1)],
+                dst_ref=slots.at[pl.ds(s * n + k, 1)],
                 send_sem=ts_sem.at[k],
                 recv_sem=tr_sem.at[s, k],
-                device_id=place(k),
+                device_id=other,
                 device_id_type=MESH,
             )
 
-        def send(k, carry):
+        for k in range(1, n):
             peak_copy(k).start()
-            return carry
-
-        def take(k, best):
+        slots[pl.ds(s * n, 1), :] = mine[0:1]
+        for k in range(1, n):
             peak_copy(k).wait_recv()
-            return jnp.maximum(best, slots[s, k])
-
-        def finish(k, carry):
-            peak_copy(k).wait_send()
-            return carry
-
-        lax.fori_loop(1, n, send, 0)
-        best = lax.fori_loop(1, n, take, own[...])
-        lax.fori_loop(1, n, finish, 0)
-        spread = lambda i: jnp.broadcast_to(best[i : i + 1, :], (8, LANES))
+        best = slots[span(s * n), :]
+        for k in range(8, n, 8):
+            best = jnp.maximum(best, slots[span(s * n + k), :])
+        best = jnp.max(best, axis=0, keepdims=True)
+        spread = lambda i: jnp.broadcast_to(best[:, i : i + 1], (8, LANES))
         bounds = [spread(i) * full(cost_ref[i]) * (1.0 / 12.0) for i in range(5)]
         total = bounds[0] * (1.0 / spacing[0])
         for i in range(1, 5):
@@ -415,54 +433,61 @@
             for copy in masks():
                 copy.wait()
 
-        for c in range(cols):
-            def move(i, carry):
-                row = c * rows * block + i * 8
-                here = span(row)
-                change = dt * h[here, :]
-                for number in range(5):
-                    change = change - scale[number] * q[number, here, :]
-                new = v[span(PAD + row), :] - change
-                new = jnp.where(t[here, :] == 1, jnp.minimum(new, -0.5), new)
-                v[span(PAD + row), :] = jnp.where(o[here, :] == 1, jnp.maximum(new, 0.5), new)
-                return carry
-
-            lax.fori_loop(0, rows * parts, move, 0, unroll=4)
-
+        def launch(c, half):
             @pl.when(s < STEPS - 1)
             def _():
-                for copy in sends(c):
-                    copy.start()
-
-            @pl.when(s == STEPS - 1)
-            def _():
-                for copy in stores(c):
-                    copy.start()
-
+                row_copy(c, 1 - half).start()
+                if half:
+                    for copy in col_copies(c):
+                        copy.start()
+
+        pending = None
+        for c in range(cols):
+            for half in range(2):
+                start = (c * rows + half * rows // 2) * block
+
+                def move(i, carry):
+                    row = start + i * 8
+                    here = span(row)
+                    change = dt * h[here, :]
+                    for number in range(5):
+                        change = change - scale[number] * q[number, here, :]
+                    new = v[span(PAD + row), :] - change
+                    new = jnp.where(t[here, :] == 1, jnp.minimum(new, -0.5), new)
+                    new = jnp.where(o[here, :] == 1, jnp.maximum(new, 0.5), new)
+                    v[span(PAD + row), :] = new
+                    out[half * rows // 2 * cols + c + i // parts * cols, span(i % parts * 8), :] = new
+                    return carry
+
+                lax.fori_loop(0, rows * parts // 2, move, 0, unroll=6)
+                if pending is not None:
+                    launch(*pending)
+                pending = (c, half)
+        launch(*pending)
+        for k in range(1, n):
+            peak_copy(k).wait_send()
         return carry
 
     lax.fori_loop(0, STEPS, step, 0)
-    for c in range(cols):
-        for copy in stores(c):
-            copy.wait()
 
 
 VMEM = pl.BlockSpec(memory_space=pltpu.VMEM)
 SMEM = pl.BlockSpec(memory_space=pltpu.SMEM)
-ANY = pl.BlockSpec(memory_space=pl.ANY)
+HBM = pl.BlockSpec(memory_space=pltpu.HBM)
 
 
 def fold(x):
     planes, rows, cols, width = x.shape
     chunks = width // LANES
-    x = x.reshape(planes, rows, cols, chunks, LANES).transpose(1, 2, 3, 0, 4)
+    x = with_layout_constraint(x.reshape(planes, rows, cols, chunks, LANES), DENSE)
+    x = x.transpose(1, 2, 3, 0, 4)
     return x.reshape(rows * cols, chunks * planes, LANES)
 
 
 def unfold(x, shape):
     planes, rows, cols, width = shape
     x = x.reshape(rows, cols, width // LANES, planes, LANES).transpose(3, 0, 1, 2, 4)
-    return x.reshape(shape)
+    return with_layout_constraint(x, DENSE).reshape(shape)
 
 
 def body(value, target, obstacle, gains, costs):
@@ -488,23 +513,30 @@
             jax.ShapeDtypeStruct((cells, block, LANES), jnp.float32),
             jax.ShapeDtypeStruct((STEPS,), jnp.float32),
         ],
-        in_specs=[SMEM, SMEM, SMEM, ANY, ANY, ANY],
-        out_specs=[ANY, SMEM],
+        in_specs=[HBM] * 6,
+        out_specs=[VMEM, SMEM],
         scratch_shapes=[
             f32(whole + 2 * PAD, LANES), i32(whole, LANES), i32(whole, LANES),
             f32(whole, LANES), f32(5, whole, LANES),
             f32(cols * 3 * block, LANES), f32(cols * 3 * block, LANES),
             f32(rows * 3 * block, LANES), f32(rows * 3 * block, LANES),
             f32(whole // planes, LANES), f32(8 * parts, LANES), f32(8 * rows * parts, LANES),
-            f32(8 * cols, LANES), f32(8 * cells, LANES), f32(8 * parts, LANES),
-            f32(8 * 12 * parts, LANES), f32(8, LANES), f32(STEPS, n, 8, LANES),
-            dma(3 * cells), dma(cells), dma(cols, 2), dma(cols, 2), dma(3, 2), dma(3, 2),
+            f32(8 * cells, LANES), f32(8 * cells, LANES), f32(8 * parts, LANES),
+            f32(8 * 12 * parts, LANES), f32(48 * UNROLL, LANES), f32(48 * UNROLL, LANES),
+            f32(8, LANES), f32(STEPS * n, LANES),
+            dma(3 * cells), dma(cols, 2), dma(cols, 2), dma(3, 2), dma(3, 2),
             dma(n), dma(STEPS, n),
+            pltpu.SemaphoreType.REGULAR((max(ny // 2 - 1 + nx // 2, 1),)),
+            pltpu.SMEM((5,), jnp.float32), pltpu.SMEM((5,), jnp.float32),
+            pltpu.SMEM(trig.shape, jnp.float32), dma(3),
         ],
         compiler_params=pltpu.CompilerParams(
             collective_id=0, has_side_effects=True, vmem_limit_bytes=40 << 20
         ),
-    )(costs, gains, trig, fold(value), fold(target), fold(obstacle))
+    )(*[
+        pltpu.with_memory_space_constraint(x, pltpu.HBM)
+        for x in (costs, gains, trig, *map(fold, (value, target, obstacle)))
+    ])
     return unfold(out, dims), steps
 
 

time: 120 us -> 91.1 us (0.76)
  Pallas kernels: 111 us -> 88.9 us
  local copies, waits for them, and re-layouts: 8.13 us -> 1.43 us
    pallas_call x1, Pallas kernels: 111 us -> 88.9 us  [body(): pl.pallas_call(functools.partial(kernel, dims, (nx, ny)), out_shape=[jax....]
    reshape x5 -> x0, local copies, waits for them, and re-layouts: 6.22 us -> none  [the longest x3 4.87 us: fold(): x = x.reshape(planes, rows, cols, chunks, LANES).transpose(1, 2, 3, 0, 4)]
where the time goes in v2:
time: 91.1 us; the launch traced here: 90.9 us
  Pallas kernels  88.9 us (98%)
  local copies, waits for them, and re-layouts  1.43 us (2%)
    pallas_call x1, Pallas kernels, body(): pl.pallas_call(functools.partial(kernel, dims, (nx, ny)), out_shape=[jax....  88.9 us

profile of v2, /device:TPU:0, one launch (start us, length us, event | category | flops | bytes accessed | tf_op | source)
XLA Modules:
  0.0 90.9 jit_solution(15503322506747403951)
XLA Ops:
  0.6 88.9 %shard_map.77 = (f32[36,48,128]{2,1,0:T(8,128)S(1)}, f32[3]{0:T(128)S(1)}) custom-call(f32[5]{0:T(128)} %cost_hbm.1, f32[5]{0:T(128)} %gain_hbm.1, f32[144]{0:T(256)} %constant.2.clone.trig_hbm, f32[36,48,128]{2,1,0:T(8,128)} %bitcast.21, s32[36,48,128]{2,1,0:T(8,128)} %bitcast.22, s32[36,48,128]{2,1,0:T(8,128)} %bitcast.23), custom_call_target="tpu_custom_call" | custom-call | tf_op jit(solution)/shard_map/pallas_call | solution.py:510
  89.5 0.9 %copy.10 = f32[4,6,6,1536]{3,0,2,1:T(4,128)} copy(f32[4,6,6,1536]{3,0,2,1:T(4,128)S(1)} %bitcast.20) | data formatting | bytes 1769472
  90.4 0.5 copy.11

commit v3 on v2

--- a/solution.py
+++ b/solution.py
@@ -97,7 +97,7 @@
     dims, sizes,
     cost_hbm, gain_hbm, trig_hbm, v_hbm, t_hbm, o_hbm,
     out, dt_ref,
-    v, t, o, h, q, ra, rb, ca, cb, f0, f1, f2, f3, f4r, f4k, keep, buf0, buf1, own, slots,
+    v, t, o, work, ra, rb, ca, cb, f0, f1, f2, f3, f4r, f4k, keep, buf0, buf1, own, slots,
     in_sem, rs_sem, rr_sem, cs_sem, cr_sem, ts_sem, tr_sem, news,
     cost_ref, gain_ref, trig_ref, small_sem,
 ):
@@ -181,8 +181,16 @@
             out.append(col_copy(c, 0))
         return out
 
-    def sends(c):
-        return [row_copy(c, 0), row_copy(c, 1)] + col_copies(c)
+    def start_row(c, turn):
+        for odd in range(2):
+
+            @pl.when(ix % 2 == odd)
+            def _():
+                row_copy(c, 1 - (turn + odd) % 2).start()
+
+    def start_cols(c):
+        for copy in col_copies(c):
+            copy.start()
 
     around = (up, down, after, before)
     barrier = pltpu.get_barrier_semaphore()
@@ -204,8 +212,9 @@
     for c in range(cols):
         for copy in loads(c):
             copy.wait()
-        for copy in sends(c):
-            copy.start()
+        start_row(c, 0)
+        start_row(c, 1)
+        start_cols(c)
     for copy in masks():
         copy.start()
 
@@ -266,8 +275,8 @@
         for p in range(planes):
             speed, part = tally(*cellsp[p], drift, kappa[0])
             top = jnp.maximum(top, speed)
-            h[spot(p), :] = part
-            q[0, spot(p), :] = cellsp[p][1]
+            work[0, spot(p), :] = part
+            work[1, spot(p), :] = cellsp[p][1]
         return top
 
     def along_lanes(slot, k, stride):
@@ -308,8 +317,8 @@
                 drift = f3[span(i * 8), :]
             speed, part = tally(middle, jump, drift, kappa[number])
             here = span(i * block + 8 * k)
-            q[number, here, :] = jump
-            h[here, :] = h[here, :] + part
+            work[1 + number, here, :] = jump
+            work[0, here, :] = work[0, here, :] + part
             return jnp.maximum(top, speed)
 
         def some(i, top):
@@ -338,8 +347,8 @@
             speed, part = tally(middle, jump, drift, kappa[2])
             top = jnp.maximum(top, speed)
             here = span((c * rows + r) * block + 8 * k)
-            h[here, :] = h[here, :] + part
-            q[2, here, :] = jump
+            work[0, here, :] = work[0, here, :] + part
+            work[3, here, :] = jump
         return top
 
     def along_rows(c, k, top):
@@ -352,8 +361,8 @@
             speed, part = tally(middle, jump, drift, kappa[1])
             top = jnp.maximum(top, speed)
             here = span((c * rows + r) * block + 8 * k)
-            h[here, :] = h[here, :] + part
-            q[1, here, :] = jump
+            work[0, here, :] = work[0, here, :] + part
+            work[2, here, :] = jump
         return top
 
     hops = [(after, before)] * (ny // 2 - 1) + [(up, down)] * (nx // 2)
@@ -374,6 +383,8 @@
                     tell(i + 1)
 
     tell(0)
+
+    order = list(range(1, n))
 
     def step(s, carry):
         tops = [None] * 5
@@ -384,6 +395,19 @@
                 top = along_lanes(slot, k, stride)(top)
                 gossip(s, slot * parts + k)
             tops[3 + slot] = top
+        @pl.when(s == 0)
+        def _():
+            for copy in masks():
+                copy.wait()
+
+            def bound(i, carry):
+                here = span(i * 8)
+                work[6, here, :] = jnp.where(t[here, :] == 1, -0.5, jnp.inf)
+                work[7, here, :] = jnp.where(o[here, :] == 1, 0.5, -jnp.inf)
+                return carry
+
+            lax.fori_loop(0, cells * parts, bound, 0, unroll=4)
+
         for c in range(3):
             for which in range(2):
                 col_copy(c if which else c + cols - 3, which).wait()
@@ -391,35 +415,37 @@
         early = zero
         for number in (0, 2, 3, 4):
             early = jnp.where(lane == number, jnp.max(tops[number]), early)
+        own[...] = early
         top = zero
         for c in range(cols):
             for which in range(2):
                 row_copy(c, which).wait()
             top = lax.fori_loop(0, parts, functools.partial(along_rows, c), top)
-        mine = jnp.where(lane == 1, jnp.max(top), early)
-        own[...] = mine
+        own[1:2, :] = jnp.max(top, axis=0, keepdims=True)
 
         def peak_copy(k):
             other = ((ix + k // ny) % nx, (iy + k % ny) % ny)
             return pltpu.make_async_remote_copy(
-                src_ref=own.at[pl.ds(0, 1)],
-                dst_ref=slots.at[pl.ds(s * n + k, 1)],
+                src_ref=own.at[pl.ds(0, 2)],
+                dst_ref=slots.at[pl.ds((s * n + k) * 2, 2)],
                 send_sem=ts_sem.at[k],
                 recv_sem=tr_sem.at[s, k],
                 device_id=other,
                 device_id_type=MESH,
             )
 
-        for k in range(1, n):
+        for k in order:
             peak_copy(k).start()
-        slots[pl.ds(s * n, 1), :] = mine[0:1]
-        for k in range(1, n):
+        slots[pl.ds(s * n * 2, 2), :] = own[0:2, :]
+        for k in order:
             peak_copy(k).wait_recv()
-        best = slots[span(s * n), :]
-        for k in range(8, n, 8):
-            best = jnp.maximum(best, slots[span(s * n + k), :])
-        best = jnp.max(best, axis=0, keepdims=True)
-        spread = lambda i: jnp.broadcast_to(best[:, i : i + 1], (8, LANES))
+        best = slots[span(s * n * 2), :]
+        for k in range(8, 2 * n, 8):
+            best = jnp.maximum(best, slots[span(s * n * 2 + k), :])
+        best = jnp.maximum(best, pltpu.roll(best, 4, 0))
+        best = jnp.maximum(best, pltpu.roll(best, 2, 0))
+        last = jnp.max(best[1:2], axis=1, keepdims=True)
+        spread = lambda i: jnp.broadcast_to(last if i == 1 else best[0:1, i : i + 1], (8, LANES))
         bounds = [spread(i) * full(cost_ref[i]) * (1.0 / 12.0) for i in range(5)]
         total = bounds[0] * (1.0 / spacing[0])
         for i in range(1, 5):
@@ -428,35 +454,46 @@
         scale = [dt * bounds[i] * (1.0 / (12.0 * spacing[i])) for i in range(5)]
         dt_ref[s] = dt[0, 0]
 
-        @pl.when(s == 0)
+        def moved(row):
+            here = span(row)
+            change = dt * work[0, here, :]
+            for number in range(5):
+                change = change - scale[number] * work[1 + number, here, :]
+            new = v[span(PAD + row), :] - change
+            return jnp.maximum(jnp.minimum(new, work[6, here, :]), work[7, here, :])
+
+        @pl.when(s == STEPS - 1)
         def _():
-            for copy in masks():
-                copy.wait()
-
-        def launch(c, half):
-            @pl.when(s < STEPS - 1)
-            def _():
-                row_copy(c, 1 - half).start()
-                if half:
-                    for copy in col_copies(c):
-                        copy.start()
-
+            def close(i, carry):
+                c, r = i // rows, i % rows
+                for k in range(parts):
+                    out[r * cols + c, 8 * k : 8 * k + 8, :] = moved(i * block + 8 * k)
+                return carry
+
+            lax.fori_loop(0, cells, close, 0)
+
+        @pl.when(s < STEPS - 1)
+        def _():
+            advance(moved)
+
+        for k in order:
+            peak_copy(k).wait_send()
+        return carry
+
+    def launch(c, half):
+        start_row(c, half)
+        if half:
+            start_cols(c)
+
+    def advance(moved):
         pending = None
         for c in range(cols):
             for half in range(2):
-                start = (c * rows + half * rows // 2) * block
+                start = (c * rows + (half + ix) % 2 * (rows // 2)) * block
 
                 def move(i, carry):
                     row = start + i * 8
-                    here = span(row)
-                    change = dt * h[here, :]
-                    for number in range(5):
-                        change = change - scale[number] * q[number, here, :]
-                    new = v[span(PAD + row), :] - change
-                    new = jnp.where(t[here, :] == 1, jnp.minimum(new, -0.5), new)
-                    new = jnp.where(o[here, :] == 1, jnp.maximum(new, 0.5), new)
-                    v[span(PAD + row), :] = new
-                    out[half * rows // 2 * cols + c + i // parts * cols, span(i % parts * 8), :] = new
+                    v[span(PAD + row), :] = moved(row)
                     return carry
 
                 lax.fori_loop(0, rows * parts // 2, move, 0, unroll=6)
@@ -464,9 +501,6 @@
                     launch(*pending)
                 pending = (c, half)
         launch(*pending)
-        for k in range(1, n):
-            peak_copy(k).wait_send()
-        return carry
 
     lax.fori_loop(0, STEPS, step, 0)
 
@@ -517,13 +551,13 @@
         out_specs=[VMEM, SMEM],
         scratch_shapes=[
             f32(whole + 2 * PAD, LANES), i32(whole, LANES), i32(whole, LANES),
-            f32(whole, LANES), f32(5, whole, LANES),
+            f32(8, whole + 8, LANES),
             f32(cols * 3 * block, LANES), f32(cols * 3 * block, LANES),
             f32(rows * 3 * block, LANES), f32(rows * 3 * block, LANES),
             f32(whole // planes, LANES), f32(8 * parts, LANES), f32(8 * rows * parts, LANES),
             f32(8 * cells, LANES), f32(8 * cells, LANES), f32(8 * parts, LANES),
             f32(8 * 12 * parts, LANES), f32(48 * UNROLL, LANES), f32(48 * UNROLL, LANES),
-            f32(8, LANES), f32(STEPS * n, LANES),
+            f32(8, LANES), f32(STEPS * n * 2, LANES),
             dma(3 * cells), dma(cols, 2), dma(cols, 2), dma(3, 2), dma(3, 2),
             dma(n), dma(STEPS, n),
             pltpu.SemaphoreType.REGULAR((max(ny // 2 - 1 + nx // 2, 1),)),

time: 91.1 us -> 88.9 us (0.976)
  Pallas kernels: 88.9 us -> 86.7 us
    pallas_call x1, Pallas kernels: 88.9 us -> 86.7 us  [body(): pl.pallas_call(functools.partial(kernel, dims, (nx, ny)), out_shape=[jax....]
where the time goes in v3:
time: 88.9 us; the launch traced here: 88.7 us
  Pallas kernels  86.7 us (98%)
  local copies, waits for them, and re-layouts  1.43 us (2%)
    pallas_call x1, Pallas kernels, body(): pl.pallas_call(functools.partial(kernel, dims, (nx, ny)), out_shape=[jax....  86.7 us

profile of v3, /device:TPU:0, one launch (start us, length us, event | category | flops | bytes accessed | tf_op | source)
XLA Modules:
  0.0 88.7 jit_solution(2269914306827609421)
XLA Ops:
  0.6 86.7 %shard_map.77 = (f32[36,48,128]{2,1,0:T(8,128)S(1)}, f32[3]{0:T(128)S(1)}) custom-call(f32[5]{0:T(128)} %cost_hbm.1, f32[5]{0:T(128)} %gain_hbm.1, f32[144]{0:T(256)} %constant.2.clone.trig_hbm, f32[36,48,128]{2,1,0:T(8,128)} %bitcast.21, s32[36,48,128]{2,1,0:T(8,128)} %bitcast.22, s32[36,48,128]{2,1,0:T(8,128)} %bitcast.23), custom_call_target="tpu_custom_call" | custom-call | tf_op jit(solution)/shard_map/pallas_call | solution.py:544
  87.3 0.9 %copy.10 = f32[4,6,6,1536]{3,0,2,1:T(4,128)} copy(f32[4,6,6,1536]{3,0,2,1:T(4,128)S(1)} %bitcast.20) | data formatting | bytes 1769472
  88.2 0.5 copy.11

commit v4 on v3

--- a/solution.py
+++ b/solution.py
@@ -464,13 +464,14 @@
 
         @pl.when(s == STEPS - 1)
         def _():
-            def close(i, carry):
-                c, r = i // rows, i % rows
-                for k in range(parts):
-                    out[r * cols + c, 8 * k : 8 * k + 8, :] = moved(i * block + 8 * k)
+            def close(c, carry):
+                for r in range(rows):
+                    for k in range(parts):
+                        row = (c * rows + r) * block + 8 * k
+                        out[r * cols + c, 8 * k : 8 * k + 8, :] = moved(row)
                 return carry
 
-            lax.fori_loop(0, cells, close, 0)
+            lax.fori_loop(0, cols, close, 0)
 
         @pl.when(s < STEPS - 1)
         def _():
@@ -496,7 +497,7 @@
                     v[span(PAD + row), :] = moved(row)
                     return carry
 
-                lax.fori_loop(0, rows * parts // 2, move, 0, unroll=6)
+                lax.fori_loop(0, rows * parts // 2, move, 0, unroll=True)
                 if pending is not None:
                     launch(*pending)
                 pending = (c, half)

time: 88.9 us -> 88.6 us (level)
  no operation moved by 1% of the time
where the time goes in v4:
time: 88.6 us; the launch traced here: 88.4 us
  Pallas kernels  86.4 us (98%)
  local copies, waits for them, and re-layouts  1.43 us (2%)
    pallas_call x1, Pallas kernels, body(): pl.pallas_call(functools.partial(kernel, dims, (nx, ny)), out_shape=[jax....  86.4 us

profile of v4, /device:TPU:0, one launch (start us, length us, event | category | flops | bytes accessed | tf_op | source)
XLA Modules:
  0.0 88.4 jit_solution(9077714867620367272)
XLA Ops:
  0.6 86.4 %shard_map.77 = (f32[36,48,128]{2,1,0:T(8,128)S(1)}, f32[3]{0:T(128)S(1)}) custom-call(f32[5]{0:T(128)} %cost_hbm.1, f32[5]{0:T(128)} %gain_hbm.1, f32[144]{0:T(256)} %constant.2.clone.trig_hbm, f32[36,48,128]{2,1,0:T(8,128)} %bitcast.21, s32[36,48,128]{2,1,0:T(8,128)} %bitcast.22, s32[36,48,128]{2,1,0:T(8,128)} %bitcast.23), custom_call_target="tpu_custom_call" | custom-call | tf_op jit(solution)/shard_map/pallas_call | solution.py:545
  87.0 0.9 %copy.10 = f32[4,6,6,1536]{3,0,2,1:T(4,128)} copy(f32[4,6,6,1536]{3,0,2,1:T(4,128)S(1)} %bitcast.20) | data formatting | bytes 1769472
  87.9 0.5 copy.11
